TPU v7x, 16 devices: a 4x2x1 block of a 4x4x8 slice. The times are simulated.
16 devices in a mesh: rep: 4 (over y, z, core), dp: 4 (over x).
Axes of the slice: x: 4, y: 2, z: 1, core: 2. Of those that a mesh axis runs over, the one named last changes fastest.
The devices are a block of a 4x4x8 slice.
Arguments:
- x: bfloat16 [16, 2048, 896], P(('rep', 'dp')), parts along dimension 0
- dy: bfloat16 [16, 2048, 896], P(('rep', 'dp')), parts along dimension 0
- w_gate: bfloat16 [2, 896, 4864], P(None, 'dp')
- w_up: bfloat16 [2, 896, 4864], P(None, 'dp')
- w_down: bfloat16 [2, 4864, 896], P(None, 'dp')
- m_w_gate: float32 [2, 896, 4864], P(None, 'dp')
- m_w_up: float32 [2, 896, 4864], P(None, 'dp')
- m_w_down: float32 [2, 4864, 896], P(None, 'dp')
- v_w_gate: float32 [2, 896, 4864], P(None, 'dp')
- v_w_up: float32 [2, 896, 4864], P(None, 'dp')
- v_w_down: float32 [2, 4864, 896], P(None, 'dp')
Outputs:
- output 1: bfloat16 [8, 896, 4864], P('rep', 'dp'), parts along dimension 0
- output 2: bfloat16 [8, 896, 4864], P('rep', 'dp'), parts along dimension 0
- output 3: bfloat16 [8, 4864, 896], P('rep', 'dp'), parts along dimension 0
- output 4: float32 [8, 896, 4864], P('rep', 'dp'), parts along dimension 0
- output 5: float32 [8, 896, 4864], P('rep', 'dp'), parts along dimension 0
- output 6: float32 [8, 4864, 896], P('rep', 'dp'), parts along dimension 0
- output 7: float32 [8, 896, 4864], P('rep', 'dp'), parts along dimension 0
- output 8: float32 [8, 896, 4864], P('rep', 'dp'), parts along dimension 0
- output 9: float32 [8, 4864, 896], P('rep', 'dp'), parts along dimension 0
There are 4 independent parts. A program takes and returns all parts, laid end to end along the dimension named above; an argument that names none is the same for every part.
All inputs are finite; a program needn't handle non-finite values.
Results may differ from a plain program's by a relative error of at most 0.022.
Values are sent between devices in bfloat16 or wider.
A program may use at most 768 MiB of HBM per device.

v0:
```python
import jax
import jax.numpy as jnp
from jax import lax
from jax.sharding import PartitionSpec as P

NAMES = ("w_gate", "w_up", "w_down")


def matmul(a, w):
    return jnp.dot(a, w, preferred_element_type=jnp.float32).astype(jnp.bfloat16)


def normed(h):
    wide = h.astype(jnp.float32)
    scale = lax.rsqrt(jnp.mean(wide**2, -1, keepdims=True) + 1e-6)
    return (wide * scale).astype(jnp.bfloat16)


def layer(h, w):
    a = normed(h)
    gate = jnp.dot(a, w["w_gate"], preferred_element_type=jnp.float32)
    up = jnp.dot(a, w["w_up"], preferred_element_type=jnp.float32)
    return h + matmul((jax.nn.silu(gate) * up).astype(jnp.bfloat16), w["w_down"])


def adamw(w, m, v, g):
    m = 0.9 * m + 0.1 * g
    v = 0.95 * v + 0.05 * g * g
    step = m * lax.rsqrt(v + 1e-8) + 0.1 * w
    return (w - 0.02 * step).astype(jnp.bfloat16), m, v


def clipped(gradients, sum_of_squares, count):
    factor = jnp.minimum(1.0, 0.5 * lax.rsqrt(sum_of_squares / count + 1e-30))
    return [g * factor for g in gradients]


def solution(mesh):
    def fetched(weights, number):
        return {name: lax.all_gather(w[number], "dp", axis=0, tiled=True) for name, w in zip(NAMES, weights, strict=True)}

    def step(x, dy, *arrays):
        weights, m, v = (arrays[i : i + 3] for i in (0, 3, 6))
        layers = weights[0].shape[0]
        h, kept = x[0], []
        for number in range(layers):
            kept.append(h)
            h = layer(h, fetched(weights, number))
        by_h, mine = dy[0], [None] * layers
        for number in reversed(range(layers)):
            _, back = jax.vjp(lambda w, h: layer(h, w), fetched(weights, number), kept[number])
            by_w, by_h = back(by_h)
            mine[number] = [lax.psum_scatter(by_w[name], "dp", scatter_dimension=0, tiled=True) for name in NAMES]
        gradients = [jnp.stack([mine[number][i] for number in range(layers)]).astype(jnp.float32) for i in range(3)]
        squares = lax.psum(sum(jnp.sum(g * g) for g in gradients), "dp")
        gradients = clipped(gradients, squares, lax.psum(1, "dp") * sum(g.size for g in gradients))
        new = [adamw(w.astype(jnp.float32), m, v, g) for w, m, v, g in zip(weights, m, v, gradients, strict=True)]
        return tuple(one[which] for which in range(3) for one in new)

    states, cut = P(("rep", "dp"), None, None), P(None, "dp", None)
    return jax.shard_map(
        step,
        mesh=mesh,
        in_specs=(states, states) + (cut,) * 9,
        out_specs=(P("rep", "dp", None),) * 9,
        check_vma=False,
    )
```

profile of v0, /device:TPU:112, one launch (start us, length us, event | category | flops | bytes accessed | tf_op | source)
XLA Modules:
  0.0 1221.9 jit_solution(2544394085038109981)
XLA Ops:
  23.5 6.1 copy.20
  32.4 6.1 copy.21
  38.4 58.5 %all-gather.13.cloned.1.call-done = bf16[1,896,4864]{2,1,0:T(8,128)(2,1)} async-done(((bf16[1,224,4864]{2,1,0:T(8,128)(2,1)}), bf16[1,896,4864]{2,1,0:T(8,128)(2,1)}) %all-gather.13.cloned.1.call-update) | async-done | bytes 8716304 | tf_op jit(solution)/shard_map/all_gather | solution.py:40
  97.0 29.2 %fusion.55 = f32[2048,4864]{1,0:T(8,128)} fusion(bf16[1,896,4864]{2,1,0:T(8,128)(2,1)} %all-gather.13.cloned.1.call-done, bf16[1,2048,896]{1,2,0:T(8,128)(2,1)} %copy.20, f32[2048]{0:T(1024)S(1)} %add_rsqrt_fusion), kind=kOutput, calls=%fused_computation.88 | convolution fusion | flops 17856462848 | bytes 52240384 | tf_op jit(solution)/shard_map/dot_general | solution.py:21
  126.2 55.9 %all-gather.15.cloned.1.call-done = bf16[1,896,4864]{2,1,0:T(8,128)(2,1)} async-done(((bf16[1,224,4864]{2,1,0:T(8,128)(2,1)}), bf16[1,896,4864]{2,1,0:T(8,128)(2,1)}) %all-gather.15.cloned.1.call-update) | async-done | bytes 8716304 | tf_op jit(solution)/shard_map/all_gather | solution.py:40
  182.1 46.4 %multiply_convert_fusion.1 = (bf16[2048,4864]{1,0:T(8,128)(2,1)}, f32[2048,4864]{1,0:T(8,128)}) fusion(f32[2048,4864]{1,0:T(8,128)} %fusion.55, bf16[1,896,4864]{2,1,0:T(8,128)(2,1)} %all-gather.15.cloned.1.call-done, bf16[1,2048,896]{1,2,0:T(8,128)(2,1)} %copy.20, f32[2048]{0:T(1024)S(1)} %add_rsqrt_fusion), kind=kOutput, calls=%fused_computation.17 | convolution fusion | flops 17916231680 | bytes 112009216 | tf_op jit(solution)/shard_map/dot_general | solution.py:22
  228.5 38.7 %all-gather.17.cloned.1.call-done = bf16[1,4864,896]{2,1,0:T(8,128)(2,1)} async-done(((bf16[1,1216,896]{2,1,0:T(8,128)(2,1)}), bf16[1,4864,896]{2,1,0:T(8,128)(2,1)}) %all-gather.17.cloned.1.call-update) | async-done | bytes 8716304 | tf_op jit(solution)/shard_map/all_gather | solution.py:40
  267.2 25.3 %fusion.61 = (f32[2048]{0:T(1024)S(1)}, bf16[2048,896]{0,1:T(8,128)(2,1)}) fusion(bf16[2048,4864]{1,0:T(8,128)(2,1)} %get-tuple-element.24, bf16[1,4864,896]{2,1,0:T(8,128)(2,1)} %all-gather.17.cloned.1.call-done, bf16[1,2048,896]{1,2,0:T(8,128)(2,1)} %copy.20), kind=kOutput, calls=%fused_computation.94 | convolution fusion | flops 17860130816 | bytes 35987456 | tf_op jit(solution)/shard_map/dot_general | solution.py:10
  293.1 59.0 %all-gather.21.cloned.1.call-done = bf16[1,4864,896]{2,1,0:T(8,128)(2,1)} async-done(((bf16[1,1216,896]{2,1,0:T(8,128)(2,1)}), bf16[1,4864,896]{2,1,0:T(8,128)(2,1)}) %all-gather.21.cloned.1.call-update) | async-done | bytes 8716304 | tf_op jit(solution)/shard_map/all_gather | solution.py:40
  352.1 28.3 %convolution_convert_fusion.1 = bf16[2048,4864]{1,0:T(8,128)(2,1)} fusion(bf16[1,4864,896]{2,1,0:T(8,128)(2,1)} %all-gather.21.cloned.1.call-done, bf16[1,2048,896]{2,1,0:T(8,128)(2,1)} %param.12), kind=kOutput, calls=%fused_computation.25 | convolution fusion | flops 17860919296 | bytes 32309248 | tf_op jit(solution)/shard_map/transpose(jvp())/dot_general | solution.py:10
  380.4 56.7 %all-gather.23.cloned.1.call-done = bf16[1,896,4864]{2,1,0:T(8,128)(2,1)} async-done(((bf16[1,224,4864]{2,1,0:T(8,128)(2,1)}), bf16[1,896,4864]{2,1,0:T(8,128)(2,1)}) %all-gather.23.cloned.1.call-update) | async-done | bytes 8716304 | tf_op jit(solution)/shard_map/all_gather | solution.py:40
  437.1 29.2 %fusion.42 = f32[2048,4864]{1,0:T(8,128)} fusion(bf16[1,896,4864]{2,1,0:T(8,128)(2,1)} %all-gather.23.cloned.1.call-done, bf16[2048,896]{0,1:T(8,128)(2,1)} %get-tuple-element.27, f32[2048]{0:T(1024)S(1)} %fusion.80), kind=kOutput, calls=%fused_computation.75 | convolution fusion | flops 17856462848 | bytes 52240384 | tf_op jit(solution)/shard_map/jvp()/dot_general | solution.py:22
  466.3 55.8 %all-gather.19.cloned.1.call-done = bf16[1,896,4864]{2,1,0:T(8,128)(2,1)} async-done(((bf16[1,224,4864]{2,1,0:T(8,128)(2,1)}), bf16[1,896,4864]{2,1,0:T(8,128)(2,1)}) %all-gather.19.cloned.1.call-update) | async-done | bytes 8716304 | tf_op jit(solution)/shard_map/all_gather | solution.py:40
  522.1 54.1 %fusion.2 = (bf16[2048,4864]{1,0:T(8,128)(2,1)}, f32[2048,4864]{1,0:T(8,128)}) fusion(f32[2048,4864]{1,0:T(8,128)} %fusion.42, bf16[2048,4864]{1,0:T(8,128)(2,1)} %convolution_convert_fusion.1, bf16[1,896,4864]{2,1,0:T(8,128)(2,1)} %all-gather.19.cloned.1.call-done, bf16[2048,896]{0,1:T(8,128)(2,1)} %get-tuple-element.27, f32[2048]{0:T(1024)S(1)} %fusion.80), kind=kOutput, calls=%fused_computation.8 | convolution fusion | flops 17976000512 | bytes 131932160 | tf_op jit(solution)/shard_map/jvp()/dot_general | solution.py:21
  576.2 29.2 %fusion.12 = bf16[2048,896]{0,1:T(8,128)(2,1)} fusion(bf16[2048,4864]{1,0:T(8,128)(2,1)} %convolution_convert_fusion.1, bf16[1,896,4864]{2,1,0:T(8,128)(2,1)} %all-gather.23.cloned.1.call-done, f32[2048,4864]{1,0:T(8,128)} %get-tuple-element.29), kind=kOutput, calls=%fused_computation.21 | convolution fusion | flops 17910726656 | bytes 72155136 | tf_op jit(solution)/shard_map/transpose(jvp())/dot_general | solution.py:22
  605.4 24.7 %fusion.63 = (f32[2048]{0:T(1024)S(1)}, bf16[2048,896]{0,1:T(8,128)(2,1)S(1)}) fusion(bf16[2048,896]{0,1:T(8,128)(2,1)S(1)} %copy-done.2, bf16[2048,896]{0,1:T(8,128)(2,1)} %fusion.12, bf16[2048,4864]{1,0:T(8,128)(2,1)} %get-tuple-element.28, bf16[1,896,4864]{2,1,0:T(8,128)(2,1)} %all-gather.19.cloned.1.call-done), kind=kOutput, calls=%fused_computation.96 | convolution fusion | flops 17860130816 | bytes 39657472 | tf_op jit(solution)/shard_map/transpose(jvp())/dot_general | solution.py:21
  634.6 26.7 %convolution_convert_fusion.2 = bf16[4864,896]{1,0:T(8,128)(2,1)} fusion(bf16[2048,4864]{1,0:T(8,128)(2,1)} %get-tuple-element.24, bf16[2048,896]{0,1:T(8,128)(2,1)S(1)} %fusion.65), kind=kOutput, calls=%fused_computation.55 | convolution fusion | flops 17855315968 | bytes 32309248 | tf_op jit(solution)/shard_map/transpose(jvp())/dot_general | solution.py:10
  661.5 35.6 %fusion.18 = bf16[4864,896]{1,0:T(8,128)(2,1)} fusion(f32[2048,4864]{1,0:T(8,128)} %fusion.42, bf16[1,2048,896]{2,1,0:T(8,128)(2,1)} %param.12, f32[2048,4864]{1,0:T(8,128)} %get-tuple-element.29), kind=kOutput, calls=%fused_computation.51 | convolution fusion | flops 17915084800 | bytes 92078080 | tf_op jit(solution)/shard_map/transpose(jvp())/dot_general | solution.py:10
  697.2 28.0 %convolution_convert_fusion = bf16[2048,4864]{1,0:T(8,128)(2,1)} fusion(bf16[2048,896]{0,1:T(8,128)(2,1)} %copy-done.3, bf16[1,4864,896]{2,1,0:T(8,128)(2,1)} %all-gather.17.cloned.1.call-done), kind=kOutput, calls=%fused_computation.24 | convolution fusion | flops 17860919296 | bytes 32309248 | tf_op jit(solution)/shard_map/transpose(jvp())/dot_general | solution.py:10
  725.2 30.3 %fusion.23 = bf16[896,4864]{1,0:T(8,128)(2,1)} fusion(bf16[2048,4864]{1,0:T(8,128)(2,1)} %convolution_convert_fusion, f32[2048,4864]{1,0:T(8,128)} %fusion.55, bf16[1,2048,896]{1,2,0:T(8,128)(2,1)} %copy.20, f32[2048]{0:T(1024)S(1)} %copy-done.9), kind=kOutput, calls=%fused_computation.54 | convolution fusion | flops 17920589824 | bytes 72163328 | tf_op jit(solution)/shard_map/transpose(jvp())/dot_general | solution.py:22
  756.2 30.4 %fusion.19 = bf16[896,4864]{1,0:T(8,128)(2,1)} fusion(bf16[2048,4864]{1,0:T(8,128)(2,1)} %convolution_convert_fusion.1, bf16[2048,896]{0,1:T(8,128)(2,1)} %get-tuple-element.27, f32[2048]{0:T(1024)S(1)} %copy-done.5, f32[2048,4864]{1,0:T(8,128)} %get-tuple-element.29), kind=kOutput, calls=%fused_computation.52 | convolution fusion | flops 17920589824 | bytes 72163328 | tf_op jit(solution)/shard_map/transpose(jvp())/dot_general | solution.py:22
  786.8 38.6 %fusion.20 = bf16[896,4864]{1,0:T(8,128)(2,1)} fusion(f32[2048,4864]{1,0:T(8,128)} %fusion.55, f32[2048,4864]{1,0:T(8,128)} %get-tuple-element.25, bf16[2048,4864]{1,0:T(8,128)(2,1)} %convolution_convert_fusion, bf16[1,2048,896]{1,2,0:T(8,128)(2,1)} %copy.20, f32[2048]{0:T(1024)S(1)} %copy-done.9), kind=kOutput, calls=%fused_computation.53 | convolution fusion | flops 17970397184 | bytes 112009216 | tf_op jit(solution)/shard_map/transpose(jvp())/dot_general | solution.py:21
  825.6 24.8 %convolution_convert_fusion.3 = bf16[896,4864]{1,0:T(8,128)(2,1)} fusion(bf16[2048,4864]{1,0:T(8,128)(2,1)} %get-tuple-element.28, bf16[2048,896]{0,1:T(8,128)(2,1)} %get-tuple-element.27, f32[2048]{0:T(1024)S(1)} %copy-done.5), kind=kOutput, calls=%fused_computation.56 | convolution fusion | flops 17856462848 | bytes 32317440 | tf_op jit(solution)/shard_map/transpose(jvp())/dot_general | solution.py:21
  850.5 5.3 fusion.32
  855.7 49.4 %reduce-scatter.11.cloned.1.call-done = bf16[224,4864]{1,0:T(8,128)(2,1)} async-done(((bf16[896,4864]{1,0:T(8,128)(2,1)}), bf16[224,4864]{1,0:T(8,128)(2,1)}) %reduce-scatter.11.cloned.1.call-update) | async-done | bytes 2179088 | tf_op jit(solution)/shard_map/reduce_scatter | solution.py:53
  905.2 81.6 %reduce-scatter.13.cloned.1.call-done = bf16[224,4864]{1,0:T(8,128)(2,1)} async-done(((bf16[896,4864]{1,0:T(8,128)(2,1)}), bf16[224,4864]{1,0:T(8,128)(2,1)}) %reduce-scatter.13.cloned.1.call-update) | async-done | bytes 2179088 | tf_op jit(solution)/shard_map/reduce_scatter | solution.py:53
  991.9 76.7 %reduce-scatter.7.cloned.1.call-done = bf16[224,4864]{1,0:T(8,128)(2,1)} async-done(((bf16[896,4864]{1,0:T(8,128)(2,1)}), bf16[224,4864]{1,0:T(8,128)(2,1)}) %reduce-scatter.7.cloned.1.call-update) | async-done | bytes 2179088 | tf_op jit(solution)/shard_map/reduce_scatter | solution.py:53
  1068.6 81.6 %reduce-scatter.9.cloned.1.call-done = bf16[224,4864]{1,0:T(8,128)(2,1)} async-done(((bf16[896,4864]{1,0:T(8,128)(2,1)}), bf16[224,4864]{1,0:T(8,128)(2,1)}) %reduce-scatter.9.cloned.1.call-update) | async-done | bytes 2179088 | tf_op jit(solution)/shard_map/reduce_scatter | solution.py:53
  1150.2 5.2 fusion.30
  1157.3 9.4 psum.7
  1167.5 18.5 %fusion.38 = (bf16[2,1216,896]{2,1,0:T(8,128)(2,1)}, f32[2,1216,896]{2,1,0:T(8,128)}, f32[2,1216,896]{2,1,0:T(8,128)}) fusion(bf16[2,1216,896]{2,1,0:T(8,128)(2,1)} %param.15, f32[]{:T(128)S(6)} %min_shard_map.3, bf16[1,1216,896]{2,1,0:T(8,128)(2,1)} %bitcast.75, bf16[1,1216,896]{2,1,0:T(8,128)(2,1)S(1)} %bitcast.73, f32[2,1216,896]{2,1,0:T(8,128)} %param.21, ...), kind=kLoop, calls=%fused_computation.71 | loop fusion | flops 43581440 | bytes 47939588 | tf_op jit(solution)/shard_map/convert_element_type | solution.py:30
  1186.0 28.8 %fusion.29 = (bf16[2,224,4864]{2,1,0:T(8,128)(2,1)}, f32[2,224,4864]{2,1,0:T(8,128)}, f32[2,224,4864]{2,1,0:T(8,128)}, bf16[2,224,4864]{2,1,0:T(8,128)(2,1)}, f3...) fusion(bf16[2,224,4864]{2,1,0:T(8,128)(2,1)S(1)} %bitcast.71, f32[]{:T(128)S(6)} %min_shard_map.3, ...), kind=kLoop, calls=%fused_computation.62 | loop fusion | flops 87162880 | bytes 95879168 | tf_op jit(solution)/shard_map/convert_element_type | solution.py:30
  (60 shorter events, 30.6 us)
Async XLA Ops:
  7.2 89.8 %all-gather.13.cloned.1.call-start = ((), (), s32[]{:S(2)}) async-start(), calls=%async_computation.12 | async-start | bytes 10895360 | tf_op jit(solution)/shard_map/all_gather | solution.py:40
  11.9 170.1 %all-gather.15.cloned.1.call-start = ((), (), s32[]{:S(2)}) async-start(), calls=%async_computation.13 | async-start | bytes 10895360 | tf_op jit(solution)/shard_map/all_gather | solution.py:40
  16.7 250.5 %all-gather.17.cloned.1.call-start = ((), (), s32[]{:S(2)}) async-start(), calls=%async_computation.14 | async-start | bytes 10895360 | tf_op jit(solution)/shard_map/all_gather | solution.py:40
  21.5 330.6 %all-gather.21.cloned.1.call-start = ((), (), s32[]{:S(2)}) async-start(), calls=%async_computation.16 | async-start | bytes 10895360 | tf_op jit(solution)/shard_map/all_gather | solution.py:40
  22.1 415.0 %all-gather.23.cloned.1.call-start = ((), (), s32[]{:S(2)}) async-start(), calls=%async_computation.17 | async-start | bytes 10895360 | tf_op jit(solution)/shard_map/all_gather | solution.py:40
  22.8 499.3 %all-gather.19.cloned.1.call-start = ((), (), s32[]{:S(2)}) async-start(), calls=%async_computation.15 | async-start | bytes 10895360 | tf_op jit(solution)/shard_map/all_gather | solution.py:40
  23.4 827.0 %reduce-scatter.15.cloned.1.call-start = ((), (), s32[]{:S(2)}) async-start(), calls=%async_computation.10 | async-start | bytes 10895360 | tf_op jit(solution)/shard_map/reduce_scatter | solution.py:53
  32.4 149.7 %copy-start.8 = (f32[2048]{0:T(1024)}, f32[2048]{0:T(1024)S(1)}, u32[]{:S(2)}) copy-start(f32[2048]{0:T(1024)S(1)} %add_rsqrt_fusion) | copy-start | bytes 24580
  292.5 0.6 copy-start.6
  293.1 337.0 %copy-start.4 = (f32[2048]{0:T(1024)}, f32[2048]{0:T(1024)S(1)}, u32[]{:S(2)}) copy-start(f32[2048]{0:T(1024)S(1)} %fusion.80) | copy-start | bytes 24580
  576.2 29.2 %copy-start.2 = (bf16[2048,896]{0,1:T(8,128)(2,1)S(1)}, bf16[2048,896]{0,1:T(8,128)(2,1)}, u32[]{:S(2)}) copy-start(bf16[2048,896]{0,1:T(8,128)(2,1)} %get-tuple-element.27) | copy-start | bytes 11010052
  605.4 24.7 %copy-start.7 = (f32[2048]{0:T(1024)S(1)}, f32[2048]{0:T(1024)}, u32[]{:S(2)}) copy-start(f32[2048]{0:T(1024)} %copy-done.6) | copy-start | bytes 24580
  605.4 24.7 %copy-start = (bf16[1,2048,896]{1,2,0:T(8,128)(2,1)S(1)}, bf16[1,2048,896]{1,2,0:T(8,128)(2,1)}, u32[]{:S(2)}) copy-start(bf16[1,2048,896]{1,2,0:T(8,128)(2,1)} %copy.21) | copy-start | bytes 11010052
  632.8 1.8 copy-start.3
  661.4 189.1 %reduce-scatter.17.cloned.1.call-start = ((), (), s32[]{:S(2)}) async-start(), calls=%async_computation.11 | async-start | bytes 10895360 | tf_op jit(solution)/shard_map/reduce_scatter | solution.py:53
  697.2 28.0 %copy-start.9 = (f32[2048]{0:T(1024)S(1)}, f32[2048]{0:T(1024)}, u32[]{:S(2)}) copy-start(f32[2048]{0:T(1024)} %copy-done.8) | copy-start | bytes 24580
  697.2 208.0 %reduce-scatter.11.cloned.1.call-start = ((), (), s32[]{:S(2)}) async-start(), calls=%async_computation.8 | async-start | bytes 10895360 | tf_op jit(solution)/shard_map/reduce_scatter | solution.py:53
  755.5 0.7 copy-start.5
  755.6 231.2 %reduce-scatter.13.cloned.1.call-start = ((), (), s32[]{:S(2)}) async-start(), calls=%async_computation.9 | async-start | bytes 10895360 | tf_op jit(solution)/shard_map/reduce_scatter | solution.py:53
  786.7 281.9 %reduce-scatter.7.cloned.1.call-start = ((), (), s32[]{:S(2)}) async-start(), calls=%async_computation.6 | async-start | bytes 10895360 | tf_op jit(solution)/shard_map/reduce_scatter | solution.py:53
  825.5 324.8 %reduce-scatter.9.cloned.1.call-start = ((), (), s32[]{:S(2)}) async-start(), calls=%async_computation.7 | async-start | bytes 10895360 | tf_op jit(solution)/shard_map/reduce_scatter | solution.py:53
  850.4 317.0 %copy-start.1 = (bf16[1216,896]{1,0:T(8,128)(2,1)S(1)}, bf16[1216,896]{1,0:T(8,128)(2,1)}, u32[]{:S(2)}) copy-start(bf16[1216,896]{1,0:T(8,128)(2,1)} %reduce-scatter.15.cloned.1.call-done) | copy-start | bytes 6537220
  1150.2 35.7 %slice-start = ((s8[4358144]{0:T(1024)(128)(4,1)}), s8[163840]{0:T(1024)(128)(4,1)S(1)}, s32[]{:S(2)}) async-start(s8[4358144]{0:T(1024)(128)(4,1)} %bitcast.70), calls=%async_computation.18 | async-start | bytes 327680
  1167.4 18.5 %slice-start.1 = ((s8[4358144]{0:T(1024)(128)(4,1)}), s8[4194304]{0:T(1024)(128)(4,1)S(1)}, s32[]{:S(2)}) async-start(s8[4358144]{0:T(1024)(128)(4,1)} %bitcast.70), calls=%async_computation.19 | async-start | bytes 8388608
Sparse Core Ops, SparseCore 0:
  12.1 84.8 all-gather.12
  99.1 82.9 all-gather.14
  184.2 82.9 all-gather.16
  269.2 82.9 all-gather.20
  354.1 82.9 all-gather.22
  439.1 82.9 all-gather.18
  661.5 80.0 reduce-scatter.14
  744.5 78.7 reduce-scatter.16
  826.3 78.7 reduce-scatter.10
  908.0 78.7 reduce-scatter.12
  989.7 78.7 reduce-scatter.6
  1071.4 78.7 reduce-scatter.8
where the time goes:
time: 1230 us; the launch traced here: 1220 us
  waiting for transfers between devices  616 us (50%)
  matrix products  481 us (39%)
  other arithmetic  68.3 us (6%)
  local copies, waits for them, and re-layouts  29.1 us (2%)
  between operations  17.3 us (1%)
    all_gather x6, waiting for transfers between devices, fetched(): lax.all_gather(w[number], 'dp', axis=0, tiled=True)  325 us
    reduce_scatter x6, waiting for transfers between devices, step(): lax.psum_scatter(by_w[name], 'dp', scatter_dimension=0, tiled=True)  289 us
    dot_general x5, matrix products, layer(): gate = jnp.dot(a, w['w_gate'], preferred_element_type=jnp.float32)  171 us
    dot_general x5, matrix products, layer(): up = jnp.dot(a, w['w_up'], preferred_element_type=jnp.float32)  165 us
    dot_general x5, matrix products, matmul(): jnp.dot(a, w, preferred_element_type=jnp.float32).astype(jnp.bfloat16)  144 us
    convert_element_type x2, other arithmetic, adamw(): return ((w - 0.02 * step).astype(jnp.bfloat16), m, v)  47.2 us
  transfers between devices with their start and end apart: 12, of which 10 were waited for; matrix products, arithmetic and copies ran while one was open for 31% of the time, Pallas kernels for 0%

commit v1 on v0

v1 whole, which is shorter than its diff:
```python
import jax
import jax.numpy as jnp
from jax import lax
from jax.experimental import pallas as pl
from jax.experimental.pallas import tpu as pltpu
from jax.sharding import PartitionSpec as P

F32, BF16 = jnp.float32, jnp.bfloat16
TILE = 256
RING = 8
KEEP = 4


def nn(a, b):
    return lax.dot_general(a, b, (((1,), (0,)), ((), ())), preferred_element_type=F32)


def nt(a, b):
    return lax.dot_general(a, b, (((1,), (1,)), ((), ())), preferred_element_type=F32)


def tn(a, b):
    return lax.dot_general(a, b, (((0,), (0,)), ((), ())), preferred_element_type=F32)


def exchange(n, tokens, d, ff, layers):
    assert n == 4 and layers == 2
    dl, fl, nt_ = d // n, ff // n, ff // TILE
    half, piece = dl // 2, fl // nt_ // 2
    quarter = piece // 2
    rows = min(512, tokens)
    NT = nt_

    def body(
        x, dy, wg, wu, wd,
        gg, gu, gd, stat, WGU, WD, DWD,
        a, aT, y, yT, h, acc, prod, dgu, wgu_v, wd_v, dw, dwd, fg, fd, og, od, own,
        l1l, l1r, l2l, l2r, l3l, l3r, k1l, k1r, k2l, k2r, k3l, k3r, sg, sd, st,
        ad_s, ad_r, ag_s, ag_r, rg_s, rg_r, rd_s, rd_r, ld, lown, lout, lst, lin, st_s, st_r,
    ):
        me, rep = lax.axis_index("dp"), lax.axis_index("rep")
        right, left, far = (lax.rem(me + k, n) for k in (1, n - 1, 2))
        core = lax.rem(rep, 2)
        R, L, O, C = {"dp": right}, {"dp": left}, {"dp": far}, {"rep": rep + 1 - 2 * core}

        def remote(src, dst, ss, rs, to):
            return lambda: pltpu.make_async_remote_copy(
                src_ref=src, dst_ref=dst, send_sem=ss, recv_sem=rs, device_id=to, device_id_type=pl.DeviceIdType.MESH
            )

        def local(src, dst, sem):
            return lambda: pltpu.make_async_copy(src, dst, sem)

        def ds(at, size, by=16):
            return pl.ds(pl.multiple_of(at, by), size)

        barrier = pltpu.get_barrier_semaphore()
        for to in (R, L, O, C):
            pl.semaphore_signal(barrier, inc=1, device_id=to, device_id_type=pl.DeviceIdType.MESH)
        pl.semaphore_wait(barrier, 4)

        def d_rows(block, j):
            return block * fl + core * (fl // 2) + j * piece

        def d_first(v):
            l, j, s = lax.div(v, NT), lax.rem(v, NT), lax.rem(v, RING)
            src, dst = wd.at[l, ds(core * (fl // 2) + j * piece, piece)], WD.at[l, ds(d_rows(me, j), piece)]
            return [remote(src, dst, ad_s.at[0, s], ad_r.at[0, s], R), remote(src, dst, ad_s.at[1, s], ad_r.at[1, s], L)]

        def d_next(v):
            l, j, s = lax.div(v, NT), lax.rem(v, NT), lax.rem(v, RING)
            lo, hi = WD.at[l, ds(d_rows(left, j), quarter)], WD.at[l, ds(d_rows(right, j) + quarter, quarter)]
            pa, pb = WD.at[l, ds(d_rows(left, j), piece)], WD.at[l, ds(d_rows(right, j), piece)]
            return [
                remote(lo, lo, ad_s.at[2, s], ad_r.at[2, s], R),
                remote(hi, hi, ad_s.at[3, s], ad_r.at[3, s], L),
                remote(pa, pa, ad_s.at[4, s], ad_r.at[4, s], C),
                remote(pb, pb, ad_s.at[5, s], ad_r.at[5, s], C),
            ]

        def d_far(v):
            l, j, s = lax.div(v, NT), lax.rem(v, NT), lax.rem(v, RING)
            pc = WD.at[l, ds(d_rows(far, j), piece)]
            return [remote(pc, pc, ad_s.at[6, s], ad_r.at[6, s], C)]

        def g_rows(block):
            return ds(block * dl + core * half, half)

        def g_first(u):
            l, j, s = lax.div(u, NT), lax.rem(u, NT), lax.rem(u, RING)
            out = []
            for k, w in enumerate((wg, wu)):
                src = w.at[l, ds(core * half, half), ds(j * TILE, TILE, TILE)]
                dst = WGU.at[l, j, g_rows(me), pl.ds(k * TILE, TILE)]
                out += [
                    remote(src, dst, ag_s.at[k, s], ag_r.at[k, s], R),
                    remote(src, dst, ag_s.at[2 + k, s], ag_r.at[2 + k, s], L),
                ]
            return out

        def g_next(u):
            l, j, s = lax.div(u, NT), lax.rem(u, NT), lax.rem(u, RING)
            lo, hi = WGU.at[l, j, g_rows(left), pl.ds(0, TILE)], WGU.at[l, j, g_rows(right), pl.ds(TILE, TILE)]
            pa, pb = WGU.at[l, j, g_rows(left)], WGU.at[l, j, g_rows(right)]
            return [
                remote(lo, lo, ag_s.at[4, s], ag_r.at[4, s], R),
                remote(hi, hi, ag_s.at[5, s], ag_r.at[5, s], L),
                remote(pa, pa, ag_s.at[6, s], ag_r.at[6, s], C),
                remote(pb, pb, ag_s.at[7, s], ag_r.at[7, s], C),
            ]

        def g_far(u):
            l, j, s = lax.div(u, NT), lax.rem(u, NT), lax.rem(u, RING)
            pc = WGU.at[l, j, g_rows(far)]
            return [remote(pc, pc, ag_s.at[8, s], ag_r.at[8, s], C)]

        def loads(l, j):
            s = lax.rem(j, 2)
            out = [
                local(wg.at[l, :, ds(j * TILE, TILE, TILE)], wgu_v.at[s, ds(me * dl, dl), pl.ds(0, TILE)], ld.at[0, s]),
                local(wu.at[l, :, ds(j * TILE, TILE, TILE)], wgu_v.at[s, ds(me * dl, dl), pl.ds(TILE, TILE)], ld.at[1, s]),
                local(WD.at[l, ds(j * TILE, TILE)], wd_v.at[s], ld.at[2, s]),
            ]
            for k, block in enumerate((right, left, far)):
                at = ds(block * dl, dl)
                out.append(local(WGU.at[l, j, at], wgu_v.at[s, at], ld.at[3 + k, s]))
            return out

        def sum_first(src, slot, land, ss, rs, size):
            return [
                remote(src(far, 0), land[0].at[slot], ss.at[0, slot], rs.at[0, slot], R),
                remote(src(far, 1), land[1].at[slot], ss.at[1, slot], rs.at[1, slot], L),
                remote(src(right, 1), land[2].at[slot], ss.at[2, slot], rs.at[2, slot], R),
                remote(src(left, 0), land[3].at[slot], ss.at[3, slot], rs.at[3, slot], L),
            ]

        def sum_next(out, slot, land, ss, rs):
            return [
                remote(out.at[lax.rem(slot, KEEP), 0], land[4].at[slot], ss.at[4, slot], rs.at[4, slot], R),
                remote(out.at[lax.rem(slot, KEEP), 1], land[5].at[slot], ss.at[5, slot], rs.at[5, slot], L),
            ]

        land_g, land_d = (l1l, l1r, l2l, l2r, l3l, l3r), (k1l, k1r, k2l, k2r, k3l, k3r)

        def rg_first(u):
            q = lax.rem(u, KEEP)
            return sum_first(lambda b, k: dw.at[q, ds(b * dl + k * half, half)], lax.rem(u, RING), land_g, rg_s, rg_r, half)

        def rg_next(u):
            return sum_next(og, lax.rem(u, RING), land_g, rg_s, rg_r)

        def rd_first(v):
            l, j = 1 - lax.div(v, NT), lax.rem(v, NT)
            at = lambda b, k: DWD.at[l, ds(b * fl + (2 * j + k) * piece, piece)]
            return sum_first(at, lax.rem(v, RING), land_d, rd_s, rd_r, piece)

        def rd_next(v):
            return sum_next(od, lax.rem(v, RING), land_d, rd_s, rd_r)

        def own_loads(v):
            l, j, s = 1 - lax.div(v, NT), lax.rem(v, NT), lax.rem(v, RING)
            at = lambda b, k, m: DWD.at[l, ds(b * fl + (2 * j + k) * piece, m * piece)]
            return [
                local(at(right, 0, 1), own.at[s, pl.ds(0, piece)], lown.at[0, s]),
                local(at(left, 1, 1), own.at[s, pl.ds(piece, piece)], lown.at[1, s]),
                local(at(me, 0, 2), own.at[s, pl.ds(2 * piece, 2 * piece)], lown.at[2, s]),
            ]

        def g_out(u):
            l, j, s = 1 - lax.div(u, NT), lax.rem(u, NT), lax.rem(u, 2)
            to = ds(j * TILE, TILE, TILE)
            return [
                local(fg.at[s, :, pl.ds(0, TILE)], gg.at[l, :, to], lout.at[0, s]),
                local(fg.at[s, :, pl.ds(TILE, TILE)], gu.at[l, :, to], lout.at[1, s]),
            ]

        def d_out(v):
            l, j, s = 1 - lax.div(v, NT), lax.rem(v, NT), lax.rem(v, 2)
            return [local(fd.at[s], gd.at[l, ds(j * 2 * piece, 2 * piece)], lout.at[2, s])]

        def dwd_out(u):
            l, j, s = 1 - lax.div(u, NT), lax.rem(u, NT), lax.rem(u, 2)
            return [local(dwd.at[s], DWD.at[l, ds(j * TILE, TILE)], lst.at[s])]

        def start(copies):
            for c in copies:
                c().start()

        def arrived(copies):
            for c in copies:
                c().wait_recv()

        def sent(copies):
            for c in copies:
                c().wait_send()

        def done(copies):
            for c in copies:
                c().wait()

        def wide(ref):
            return ref.astype(F32)

        tF = NT + 8
        tL, tB, tE = tF + NT, tF + 2 * NT, tF + 3 * NT
        end = tE + NT + 5
        blk = min(256, tokens)
        nblk = tokens // blk

        own_w = [local(wd.at[l], buf, lin.at[l]) for l, buf in ((0, y.at[pl.ds(0, fl)]), (1, h.at[pl.ds(0, fl)]))]
        put_w = [local(buf, WD.at[l, ds(me * fl, fl)], lin.at[l]) for l, buf in ((0, y.at[pl.ds(0, fl)]), (1, h.at[pl.ds(0, fl)]))]
        own_x = [local(x, h, lin.at[2]), local(dy, y, lin.at[3])]

        def norm_into(l, r):
            hw = wide(h[r, :])
            scale = lax.rsqrt(jnp.mean(hw * hw, -1, keepdims=True) + 1e-6)
            n_ = (hw * scale).astype(BF16)
            a[l, r, :] = n_
            aT[l, :, r] = n_.T

        def loop(t, _):
            def at(t0, count, f):
                k = t - t0

                @pl.when((k >= 0) & (k < count))
                def _():
                    f(k)

            at(8, 2 * NT, lambda v: sent(d_first(v) + d_next(v) + d_far(v)))
            at(tF + 1, 2 * NT, lambda u: sent(g_first(u) + g_next(u) + g_far(u)))
            at(0, 2 * NT, lambda v: start(d_first(v)))
            at(tF - 4, 2 * NT, lambda u: start(g_first(u)))
            at(tL + 1, 2 * NT, lambda u: start(rg_first(u)))
            at(tB + 1, 2 * NT, lambda v: start(rd_first(v) + own_loads(v)))

            @pl.when(t == 0)
            def _():
                start(own_w)

            @pl.when(t == 1)
            def _():
                done(own_w)
                start(put_w)

            @pl.when(t == 2)
            def _():
                done(put_w)
                start(own_x)
                acc[...] = jnp.zeros_like(acc)
                sg[...] = jnp.zeros_like(sg)
                sd[...] = jnp.zeros_like(sd)

            @pl.when(t == 3)
            def _():
                done(own_x)

            def begin(m):
                r = ds(m * blk, blk, blk)
                norm_into(0, r)
                yT[:, r] = y[r, :].T

            at(4, nblk, begin)

            def d_pass(v):
                arrived(d_first(v))
                start(d_next(v))

            def d_last(v):
                arrived(d_next(v)[:2])
                start(d_far(v))

            at(3, 2 * NT, d_pass)
            at(6, 2 * NT, d_last)
            at(7, 2 * NT, lambda v: arrived(d_next(v)[2:] + d_far(v)))

            @pl.when(t == tL)
            def _():
                def piece_(m, _):
                    r = ds(m * blk, blk, blk)
                    h[r, :] = (wide(h[r, :]) + wide(acc[r, :].astype(BF16))).astype(BF16)
                    acc[r, :] = jnp.zeros((blk, d), F32)
                    norm_into(1, r)
                    return 0

                lax.fori_loop(0, nblk, piece_, 0)

            @pl.when(t == tB)
            def _():
                def piece_(m, _):
                    r = ds(m * blk, blk, blk)
                    hw, da = wide(h[r, :]), wide(acc[r, :].astype(BF16))
                    scale = lax.rsqrt(jnp.mean(hw * hw, -1, keepdims=True) + 1e-6)
                    by_scale = jnp.sum(da * hw, -1, keepdims=True)
                    by_h = (da * scale - hw * (by_scale * scale * scale * scale * (1.0 / d))).astype(BF16)
                    by = (wide(y[r, :]) + wide(by_h)).astype(BF16)
                    y[r, :] = by
                    yT[:, r] = by.T
                    return 0

                lax.fori_loop(0, nblk, piece_, 0)

            def forward(j):
                s = lax.rem(j, 2)
                done(loads(0, j))

                def part(m, _):
                    r = ds(m * rows, rows, rows)
                    both = nn(a[0, r, :], wgu_v[s])
                    gate, up = both[:, :TILE], both[:, TILE:]
                    p = (gate * (1 / (1 + jnp.exp(-gate))) * up).astype(BF16)
                    acc[r, :] += nn(p, wd_v[s])
                    return 0

                lax.fori_loop(0, tokens // rows, part, 0)

            at(tF, NT, forward)

            def back_1(u):
                l, s = 1 - lax.div(u, NT), lax.rem(lax.rem(u, NT), 2)
                done(loads(l, lax.rem(u, NT)))

                def part(m, _):
                    r = ds(m * rows, rows, rows)
                    both = nn(a[l, r, :], wgu_v[s])
                    gate, up = both[:, :TILE], both[:, TILE:]
                    by = wide(nt(y[r, :], wd_v[s]).astype(BF16))
                    sig = 1 / (1 + jnp.exp(-gate))
                    act = gate * sig
                    prod[r, :] = (act * up).astype(BF16)
                    dgu[r, TILE:] = (by * act).astype(BF16)
                    dgu[r, :TILE] = (by * up * (sig * (1 + gate * (1 - sig)))).astype(BF16)
                    return 0

                lax.fori_loop(0, tokens // rows, part, 0)

            at(tL, 2 * NT, back_1)

            def g_pass(u):
                arrived(g_first(u))
                start(g_next(u))

            def g_last(u):
                arrived(g_next(u)[:2])
                start(g_far(u))

            at(tF - 2, 2 * NT, g_pass)
            at(tF - 1, 2 * NT, g_last)

            def back_2(u):
                l, q = 1 - lax.div(u, NT), lax.rem(u, KEEP)

                def part(m, _):
                    r = ds(m * dl, dl)
                    dw[q, r, :] = nn(aT[l, r, :], dgu[...]).astype(BF16)
                    return 0

                lax.fori_loop(0, n, part, 0)

            at(tL, 2 * NT, back_2)

            def add_g(u):
                s, q = lax.rem(u, RING), lax.rem(u, KEEP)
                o = lax.rem(s, KEEP)
                arrived(rg_first(u)[:2])
                og[o, 0] = (wide(l1l[s]) + wide(dw[q, ds(right * dl, half), :])).astype(BF16)
                og[o, 1] = (wide(l1r[s]) + wide(dw[q, ds(left * dl + half, half), :])).astype(BF16)
                start(rg_next(u))

            def add_d(v):
                s = lax.rem(v, RING)
                o = lax.rem(s, KEEP)
                arrived(rd_first(v)[:2])
                done(own_loads(v)[:2])
                od[o, 0] = (wide(k1l[s]) + wide(own[s, pl.ds(0, piece), :])).astype(BF16)
                od[o, 1] = (wide(k1r[s]) + wide(own[s, pl.ds(piece, piece), :])).astype(BF16)
                start(rd_next(v))

            at(tL + 2, 2 * NT, add_g)
            at(tB + 3, 2 * NT, add_d)

            def back_3(u):
                at_, s = dwd_out(u), lax.rem(u, 2)
                dwd[s] = tn(prod[...], y[...]).astype(BF16)
                start(at_)

            at(tL, 2 * NT, back_3)
            at(tL + 1, 2 * NT, lambda u: done(dwd_out(u)))

            def back_4(u):
                s = lax.rem(u, 2)

                def part(m, _):
                    r = ds(m * rows, rows, rows)
                    acc[r, :] += nt(dgu[r, :], wgu_v[s])
                    return 0

                lax.fori_loop(0, tokens // rows, part, 0)

            at(tL, NT, back_4)

            at(tF - 1, 2 * NT, lambda u: arrived(g_next(u)[2:] + g_far(u)))

            k = t + 1 - tF

            @pl.when((k >= 0) & (k < 3 * NT))
            def _():
                start(loads(lax.rem(lax.div(k, NT), 2), lax.rem(k, NT)))

            def total_g(u):
                s, q, f = lax.rem(u, RING), lax.rem(u, KEEP), lax.rem(u, 2)
                arrived(rg_first(u)[2:] + rg_next(u))
                lo = wide(dw[q, ds(me * dl, half), :]) + wide(l3l[s]) + wide(l2r[s])
                hi = wide(dw[q, ds(me * dl + half, half), :]) + wide(l3r[s]) + wide(l2l[s])
                lo, hi = lo.astype(BF16), hi.astype(BF16)
                fg[f, pl.ds(0, half), :] = lo
                fg[f, pl.ds(half, half), :] = hi
                lo, hi = wide(lo), wide(hi)
                sg[...] += jnp.sum((lo * lo + hi * hi).reshape(half // 8, 8, 2 * TILE), 0)
                start(g_out(u))
                sent(rg_first(u) + rg_next(u))

            def total_d(v):
                s, f = lax.rem(v, RING), lax.rem(v, 2)
                arrived(rd_first(v)[2:] + rd_next(v))
                done(own_loads(v)[2:])
                lo = wide(own[s, pl.ds(2 * piece, piece), :]) + wide(k3l[s]) + wide(k2r[s])
                hi = wide(own[s, pl.ds(3 * piece, piece), :]) + wide(k3r[s]) + wide(k2l[s])
                lo, hi = lo.astype(BF16), hi.astype(BF16)
                fd[f, pl.ds(0, piece), :] = lo
                fd[f, pl.ds(piece, piece), :] = hi
                lo, hi = wide(lo), wide(hi)
                sd[...] += jnp.sum((lo * lo + hi * hi).reshape(piece // 8, 8, d), 0)
                start(d_out(v))
                sent(rd_first(v) + rd_next(v))

            at(tL + 4, 2 * NT, lambda u: done(g_out(u)))
            at(tL + 3, 2 * NT, total_g)
            at(tB + 6, 2 * NT, lambda v: done(d_out(v)))
            at(tB + 5, 2 * NT, total_d)
            return 0

        lax.fori_loop(0, end + 1, loop, 0)

        parts = [sg[:, k * 128 : (k + 1) * 128] for k in range(2 * TILE // 128)] + [sd[:, k * 128 : (k + 1) * 128] for k in range(d // 128)]
        st[3] = sum(parts[1:], parts[0])
        sends = [remote(st.at[3], st.at[k], st_s.at[k], st_r.at[k], to) for k, to in enumerate((R, L, O))]
        start(sends)
        done(sends)
        st[4] = st[0] + st[1] + st[2] + st[3]
        last = [local(st.at[4], stat, lin.at[0])]
        start(last)
        done(last)

    any_ = pl.BlockSpec(memory_space=pl.ANY)
    shapes = [
        ((layers, dl, ff), BF16), ((layers, dl, ff), BF16), ((layers, fl, d), BF16), ((8, 128), F32),
        ((layers, NT, d, 2 * TILE), BF16), ((layers, ff, d), BF16), ((layers, ff, d), BF16),
    ]
    V, S = pltpu.VMEM, pltpu.SemaphoreType.DMA
    scratch = [
        V((layers, tokens, d), BF16), V((layers, d, tokens), BF16), V((tokens, d), BF16), V((d, tokens), BF16), V((tokens, d), BF16),
        V((tokens, d), F32), V((tokens, TILE), BF16), V((tokens, 2 * TILE), BF16),
        V((2, d, 2 * TILE), BF16), V((2, TILE, d), BF16), V((KEEP, d, 2 * TILE), BF16), V((2, TILE, d), BF16),
        V((2, dl, 2 * TILE), BF16), V((2, 2 * piece, d), BF16), V((KEEP, 2, half, 2 * TILE), BF16), V((KEEP, 2, piece, d), BF16),
        V((RING, 4 * piece, d), BF16),
    ]
    scratch += [V((RING, half, 2 * TILE), BF16)] * 6 + [V((RING, piece, d), BF16)] * 6
    scratch += [V((8, 2 * TILE), F32), V((8, d), F32), V((5, 8, 128), F32)]
    scratch += [S((7, RING)), S((7, RING)), S((9, RING)), S((9, RING)), S((6, RING)), S((6, RING)), S((6, RING)), S((6, RING))]
    scratch += [S((6, 2)), S((3, RING)), S((3, 2)), S((2,)), S((4,)), S((3,)), S((3,))]
    return pl.pallas_call(
        body,
        out_shape=[jax.ShapeDtypeStruct(*s) for s in shapes],
        in_specs=[any_] * 5,
        out_specs=[any_] * 7,
        scratch_shapes=scratch,
        compiler_params=pltpu.CompilerParams(collective_id=0, has_side_effects=True, vmem_limit_bytes=67043328),
        name="exchange",
    )


def adamw(w, m, v, g):
    m = 0.9 * m + 0.1 * g
    v = 0.95 * v + 0.05 * g * g
    step = m * lax.rsqrt(v + 1e-8) + 0.1 * w
    return (w - 0.02 * step).astype(BF16), m, v


def solution(mesh):
    n = mesh.shape["dp"]

    def step(x, dy, *arrays):
        weights, m, v = (arrays[i : i + 3] for i in (0, 3, 6))
        layers, ff, d = weights[2].shape[0], weights[2].shape[1] * n, weights[2].shape[2]
        *gradients, stat = exchange(n, x.shape[1], d, ff, layers)(x[0], dy[0], *weights)[:4]
        count = n * sum(g.size for g in gradients)
        factor = jnp.minimum(1.0, 0.5 * lax.rsqrt(jnp.sum(stat) / count + 1e-30))
        new = [adamw(w.astype(F32), m, v, g.astype(F32) * factor) for w, m, v, g in zip(weights, m, v, gradients, strict=True)]
        return tuple(one[which] for which in range(3) for one in new)

    states, cut = P(("rep", "dp"), None, None), P(None, "dp", None)
    return jax.shard_map(
        step,
        mesh=mesh,
        in_specs=(states, states) + (cut,) * 9,
        out_specs=(P("rep", "dp", None),) * 9,
        check_vma=False,
    )
```

time: 1230 us -> 795 us (0.65)
  Pallas kernels: 0 us -> 740 us
  waiting for transfers between devices: 616 us -> 0 us
  matrix products: 481 us -> 0 us
  local copies, waits for them, and re-layouts: 29.1 us -> 0.01 us
  other arithmetic: 68.3 us -> 52 us
  between operations: 17.3 us -> 1.41 us
    pallas_call x0 -> x1, Pallas kernels: none -> 740 us  [step(): exchange(n, x.shape[1], d, ff, layers)(x[0], dy[0], *weights)[:4]]
    dot_general x15 -> x0, matrix products: 481 us -> none  [the longest x5 171 us: layer(): gate = jnp.dot(a, w['w_gate'], preferred_element_type=jnp.float32)]
    all_gather x6 -> x0, waiting for transfers between devices: 325 us -> none  [fetched(): lax.all_gather(w[number], 'dp', axis=0, tiled=True)]
    reduce_scatter x6 -> x0, waiting for transfers between devices: 289 us -> none  [step(): lax.psum_scatter(by_w[name], 'dp', scatter_dimension=0, tiled=True)]
    reduce_sum x4 -> x1, other arithmetic: 18.3 us -> 1.27 us  [step(): factor = jnp.minimum(1.0, 0.5 * lax.rsqrt(jnp.sum(stat) / count + 1e-30))]
    unnamed x26 -> x2, local copies, waits for them, and re-layouts: 15.1 us -> 0.01 us
    slice x3 -> x0, local copies, waits for them, and re-layouts: 13.9 us -> none  [fetched(): w[number]]
  transfers between devices with their start and end apart: 12 -> 0, of which waited for: 10 -> 0; matrix products, arithmetic and copies ran while one was open for 31% -> 0% of each run, Pallas kernels for 0% -> 0%
where the time goes in v1:
time: 795 us; the launch traced here: 794 us
  Pallas kernels  740 us (93%)
  other arithmetic  52 us (7%)
    pallas_call x1, Pallas kernels, step(): exchange(n, x.shape[1], d, ff, layers)(x[0], dy[0], *weights)[:4]  740 us
    convert_element_type x2, other arithmetic, adamw(): return ((w - 0.02 * step).astype(BF16), m, v)  50.7 us

profile of v1, /device:TPU:112, one launch (start us, length us, event | category | flops | bytes accessed | tf_op | source)
XLA Modules:
  0.0 793.6 jit_solution(7472720302700346994)
XLA Ops:
  0.6 740.2 %exchange.1 = (bf16[2,224,4864]{2,1,0:T(8,128)(2,1)}, bf16[2,224,4864]{2,1,0:T(8,128)(2,1)}, bf16[2,1216,896]{2,1,0:T(8,128)(2,1)}, f32[8,128]{1,0:T(8,128)}, bf...) custom-call(bf16[2048,896]{1,0:T(8,128)(2,1)} %bitcast.2, ...), custom_call_target="tpu_custom_call" | custom-call | tf_op jit(solution)/shard_map/exchange/pallas_call | solution.py:495
  740.8 1.3 reduce_sum.9
  742.8 0.0 copy-start
  742.8 18.9 %fusion.8 = (bf16[2,1216,896]{2,1,0:T(8,128)(2,1)}, f32[2,1216,896]{2,1,0:T(8,128)}, f32[2,1216,896]{2,1,0:T(8,128)}) fusion(bf16[2,1216,896]{2,1,0:T(8,128)(2,1)} %wd.1, f32[]{:T(128)S(6)} %min_shard_map.3, bf16[2,1216,896]{2,1,0:T(8,128)(2,1)} %get-tuple-element.16, f32[2,1216,896]{2,1,0:T(8,128)} %param.21, f32[2,1216,896]{2,1,0:T(8,128)} %param.18), kind=kLoop, calls=%fused_computation.17 | loop fusion | flops 37044224 | bytes 47939588 | tf_op jit(solution)/shard_map/convert_element_type | solution.py:486
  761.7 0.0 copy-done
  761.7 31.8 %fusion.2 = (bf16[2,224,4864]{2,1,0:T(8,128)(2,1)}, f32[2,224,4864]{2,1,0:T(8,128)}, f32[2,224,4864]{2,1,0:T(8,128)}, bf16[2,224,4864]{2,1,0:T(8,128)(2,1)}, f32...) fusion(bf16[2,224,4864]{2,1,0:T(8,128)(2,1)S(1)} %copy-done, f32[]{:T(128)S(6)} %min_shard_map.3, ...), kind=kLoop, calls=%fused_computation.11 | loop fusion | flops 74088448 | bytes 95879168 | tf_op jit(solution)/shard_map/convert_element_type | solution.py:486
Async XLA Ops:
  742.8 18.9 %copy-start = (bf16[2,224,4864]{2,1,0:T(8,128)(2,1)S(1)}, bf16[2,224,4864]{2,1,0:T(8,128)(2,1)}, u32[]{:S(2)}) copy-start(bf16[2,224,4864]{2,1,0:T(8,128)(2,1)} %wg.1) | copy-start | bytes 13074436

commit v2 on v1

v2 whole, which is shorter than its diff:
```python
import jax
import jax.numpy as jnp
from jax import lax
from jax.experimental import pallas as pl
from jax.experimental.pallas import tpu as pltpu
from jax.sharding import PartitionSpec as P

F32, BF16 = jnp.float32, jnp.bfloat16
TILE = 256
RING = 8
TURNS = 12
KEEP = 5
HELD = 4


def nn(a, b):
    return lax.dot_general(a, b, (((1,), (0,)), ((), ())), preferred_element_type=F32)


def nt(a, b):
    return lax.dot_general(a, b, (((1,), (1,)), ((), ())), preferred_element_type=F32)


def exchange(n, tokens, d, ff, layers):
    assert n == 4 and layers == 2
    dl, fl, nt_ = d // n, ff // n, ff // TILE
    half, piece = dl // 2, fl // nt_ // 2
    lent = (half * 3 // 7, half // 2)
    lent_d = (0, piece // 2)
    rows, span = min(512, tokens), min(1024, tokens)
    late = 5
    NT = nt_
    m4 = NT - 3
    assert m4 % 4 == 0 and ff == n * NT * 64

    def tile(j):
        return jnp.where(j < m4, (m4 // 4 + 1) * lax.rem(j, 4) + lax.div(j, 4), (m4 // 4 + 1) * (j - m4) + m4 // 4)

    def unit(block, v):
        return jnp.where(v < m4, block + v, jnp.where(v - m4 < block, v - m4, v))

    def body(
        x, dy, wg, wu, wd,
        gg, gu, gd, stat, WGU, WD, DWD,
        a, aT, y, yT, h, acc, prod, dgu, wgu_v, wd_v, dw, dwd, fg, fd, og, od, own,
        l1l, l1r, l2l, l2r, l3l, l3r, k1l, k1r, k2l, k2r, k3l, k3r, sg, sd, st,
        ad_1, ad_n, ad_a, ad_b, ag_1, ag_n, ag_a, ag_b, rg_s, rg_a, rg_b, rd_s, rd_a, rd_b, ld, lown, lout, lst, lin, st_s, st_r,
    ):
        me, rep = lax.axis_index("dp"), lax.axis_index("rep")
        right, left, far = (lax.rem(me + k, n) for k in (1, n - 1, 2))
        core = lax.rem(rep, 2)
        chip = lax.rem(lax.div(rep, 2), 2)
        R, L, O, C, Y = {"dp": right}, {"dp": left}, {"dp": far}, {"rep": rep + 1 - 2 * core}, {"rep": rep + 2 - 4 * chip}

        def remote(src, dst, ss, rs, to):
            return lambda: pltpu.make_async_remote_copy(
                src_ref=src, dst_ref=dst, send_sem=ss, recv_sem=rs, device_id=to, device_id_type=pl.DeviceIdType.MESH
            )

        def local(src, dst, sem):
            return lambda: pltpu.make_async_copy(src, dst, sem)

        def ds(at, size, by=16):
            return pl.ds(pl.multiple_of(at, by), size)

        barrier = pltpu.get_barrier_semaphore()
        for to in (R, L, O, C, Y):
            pl.semaphore_signal(barrier, inc=1, device_id=to, device_id_type=pl.DeviceIdType.MESH)
        pl.semaphore_wait(barrier, 5)

        def take_g(rows_, sem):
            pltpu.make_async_copy(WGU.at[0, 0, pl.ds(0, rows_)], WGU.at[0, 0, pl.ds(0, rows_)], sem).wait()

        def take_d(rows_, sem):
            pltpu.make_async_copy(WD.at[0, pl.ds(0, rows_)], WD.at[0, pl.ds(0, rows_)], sem).wait()

        class Way:
            def __init__(self, take, first, pass_on, share, whole, got, sent_a, sent_b, sizes):
                lo, hi = pass_on
                self.take, self.got, self.sent_a, self.sent_b, self.sizes = take, got, sent_a, sent_b, sizes
                self.first = [remote(src, dst, sent_a, got[0], to) for src, dst, to in first]
                self.second = [remote(lo, lo, sent_b, got[1], R), remote(hi, hi, sent_b, got[1], L)]
                self.across = [remote(share(b), share(b), sent_b, got[2], Y) for b in (left, right, far)] if sizes[2] else []
                self.inside = [remote(whole(b), whole(b), sent_b, got[3], C) for b in (left, right, far)]

            def go(self, step):
                if step and self.sizes[step - 1]:
                    self.take(self.sizes[step - 1], self.got[step - 1])
                start(((), self.second + self.across[:2], self.across[2:], self.inside, ())[step] if step else self.first)

            def sent_first(self):
                self.take(self.sizes[0], self.sent_a)

            def sent_rest(self):
                self.take(sum(self.sizes[1:]), self.sent_b)

        def d_in(l, j):
            s, few = lax.rem(l * (NT + 1) + j, TURNS), lent_d[l]
            most = piece - few

            def rows_of(block, at, size):
                return ds(block * fl + (2 * unit(block, j) + core) * piece + at, size, 8)

            mine = wd.at[l, ds((2 * unit(me, j) + core) * piece + chip * few, most)]
            to = WD.at[l, rows_of(me, chip * few, most)]
            lo = WD.at[l, rows_of(left, chip * few, most // 2)]
            hi = WD.at[l, rows_of(right, chip * few + most // 2, most // 2)]
            share = lambda b: WD.at[l, rows_of(b, chip * most, few)]
            whole = lambda b: WD.at[l, rows_of(b, 0, piece)]
            got = [ad_1.at[j]] + [ad_n.at[i, s] for i in range(3)]
            sizes = (2 * most, most, 3 * few, 3 * piece)
            return Way(take_d, [(mine, to, R), (mine, to, L)], (lo, hi), share, whole, got, ad_a.at[l, lax.rem(j, TURNS)], ad_b.at[s], sizes)

        def g_in(l, j):
            s, few = lax.rem(l * NT + j, TURNS), lent[l]
            most = half - few

            def rows_of(block, at, size):
                return ds(block * dl + core * half + at, size, 8)

            first = []
            for k, w in enumerate((wg, wu)):
                src = w.at[l, ds(core * half + chip * few, most, 8), ds(tile(j) * TILE, TILE, TILE)]
                dst = WGU.at[l, j, rows_of(me, chip * few, most), pl.ds(k * TILE, TILE)]
                first += [(src, dst, R), (src, dst, L)]
            lo = WGU.at[l, j, rows_of(left, chip * few, most), pl.ds(0, TILE)]
            hi = WGU.at[l, j, rows_of(right, chip * few, most), pl.ds(TILE, TILE)]
            share = lambda b: WGU.at[l, j, rows_of(b, chip * most, few)]
            whole = lambda b: WGU.at[l, j, rows_of(b, 0, half)]
            got = [ag_1.at[j]] + [ag_n.at[i, s] for i in range(3)]
            sizes = (2 * most, most, 3 * few, 3 * half)
            return Way(take_g, first, (lo, hi), share, whole, got, ag_a.at[l, lax.rem(j, TURNS)], ag_b.at[s], sizes)

        def loads(l, j, k):
            s = lax.rem(k, 2)
            out = [
                local(wg.at[l, :, ds(tile(j) * TILE, TILE, TILE)], wgu_v.at[s, ds(me * dl, dl), pl.ds(0, TILE)], ld.at[s]),
                local(wu.at[l, :, ds(tile(j) * TILE, TILE, TILE)], wgu_v.at[s, ds(me * dl, dl), pl.ds(TILE, TILE)], ld.at[s]),
                local(WD.at[l, ds(tile(j) * TILE, TILE)], wd_v.at[s], ld.at[s]),
            ]
            for block in (right, left, far):
                at = ds(block * dl, dl)
                out.append(local(WGU.at[l, j, at], wgu_v.at[s, at], ld.at[s]))
            return out

        def loaded(k):
            take_d(3 * TILE, ld.at[lax.rem(k, 2)])

        def sum_first(src, slot, land, ss, ra, rb):
            return [
                remote(src(far, 0), land[0].at[slot], ss.at[slot], ra.at[slot], R),
                remote(src(far, 1), land[1].at[slot], ss.at[slot], ra.at[slot], L),
                remote(src(right, 1), land[2].at[slot], ss.at[slot], rb.at[slot], R),
                remote(src(left, 0), land[3].at[slot], ss.at[slot], rb.at[slot], L),
            ]

        def sum_next(out, slot, land, ss, rb):
            return [
                remote(out.at[lax.rem(slot, HELD), 0], land[4].at[slot], ss.at[slot], rb.at[slot], R),
                remote(out.at[lax.rem(slot, HELD), 1], land[5].at[slot], ss.at[slot], rb.at[slot], L),
            ]

        land_g, land_d = (l1l, l1r, l2l, l2r, l3l, l3r), (k1l, k1r, k2l, k2r, k3l, k3r)

        def rg_first(u):
            q = lax.rem(u, KEEP)
            return sum_first(lambda b, k: dw.at[q, ds(b * dl + k * half, half)], lax.rem(u, RING), land_g, rg_s, rg_a, rg_b)

        def rg_next(u):
            return sum_next(og, lax.rem(u, RING), land_g, rg_s, rg_b)

        def rd_first(v):
            l, j = 1 - lax.div(v, NT), lax.rem(v, NT)
            at = lambda b, k: DWD.at[l, ds(b * fl + (2 * unit(b, j) + k) * piece, piece)]
            return sum_first(at, lax.rem(v, RING), land_d, rd_s, rd_a, rd_b)

        def rd_next(v):
            return sum_next(od, lax.rem(v, RING), land_d, rd_s, rd_b)

        def own_loads(v):
            l, j, s = 1 - lax.div(v, NT), lax.rem(v, NT), lax.rem(v, RING)
            at = lambda b, k, m: DWD.at[l, ds(b * fl + (2 * unit(b, j) + k) * piece, m * piece)]
            return [
                local(at(right, 0, 1), own.at[s, pl.ds(0, piece)], lown.at[0, s]),
                local(at(left, 1, 1), own.at[s, pl.ds(piece, piece)], lown.at[0, s]),
                local(at(me, 0, 2), own.at[s, pl.ds(2 * piece, 2 * piece)], lown.at[1, s]),
            ]

        def g_out(u):
            l, j, s = 1 - lax.div(u, NT), lax.rem(u, NT), lax.rem(u, 2)
            to = ds(tile(j) * TILE, TILE, TILE)
            return [
                local(fg.at[s, :, pl.ds(0, TILE)], gg.at[l, :, to], lout.at[0, s]),
                local(fg.at[s, :, pl.ds(TILE, TILE)], gu.at[l, :, to], lout.at[0, s]),
            ]

        def d_out(v):
            l, j, s = 1 - lax.div(v, NT), lax.rem(v, NT), lax.rem(v, 2)
            return [local(fd.at[s], gd.at[l, ds(unit(me, j) * 2 * piece, 2 * piece)], lout.at[1, s])]

        def dwd_out(u):
            l, j, s = 1 - lax.div(u, NT), lax.rem(u, NT), lax.rem(u, 2)
            return [local(dwd.at[s], DWD.at[l, ds(tile(j) * TILE, TILE)], lst.at[s])]

        def start(copies):
            for c in copies:
                c().start()

        def done(copies):
            for c in copies:
                c().wait()

        def wide(ref):
            return ref.astype(F32)

        tF = 7
        tL, tB, tE = tF + NT, tF + 2 * NT, tF + 3 * NT
        end = tE + 9
        blk = min(256, tokens)
        nblk = tokens // blk

        aside = a.at[1, pl.ds(0, fl)]
        own_w = [[local(wd.at[l], aside, lin.at[0])] for l in range(layers)]
        put_w = [[local(aside, WD.at[l, ds(me * fl, fl)], lin.at[0])] for l in range(layers)]
        own_x = [local(x, h, lin.at[1]), local(dy, y, lin.at[2])]

        def norm_into(l, r):
            hw = wide(h[r, :])
            scale = lax.rsqrt(jnp.mean(hw * hw, -1, keepdims=True) + 1e-6)
            n_ = (hw * scale).astype(BF16)
            a[l, r, :] = n_
            aT[l, :, r] = n_.T

        def loop(t, _):
            def at(t0, count, f):
                k = t - t0

                @pl.when((k >= 0) & (k < count))
                def _():
                    f(k)

            def ramp(ahead, more, f, late=0):
                lo, hi = (jnp.clip(s - tF + ahead + jnp.clip(s - tF - late, 0, more), 0, NT) for s in (t, t + 1))

                @pl.when(hi > lo)
                def _():
                    def one(j, _):
                        f(j)
                        return 0

                    lax.fori_loop(lo, hi, one, 0)

            def at4(t0, f):
                k = t - t0

                @pl.when((k >= 0) & (k < NT) & (lax.rem(k, 4) == 0))
                def _():
                    def one(v, _):
                        f(v)
                        return 0

                    lax.fori_loop(k, jnp.minimum(k + 4, NT), one, 0)

            at(tF - 4, NT, lambda j: g_in(0, j).sent_first())
            at4(tF - 4, lambda j: d_in(0, j).sent_first())
            for l in range(layers):
                at(tF + l * NT + 1, NT, lambda j: g_in(l, j).sent_rest())
                at4(tF + l * NT, lambda j: d_in(l, j).sent_rest())
            at4(tF - 7, lambda j: d_in(0, j).go(0))
            ramp(6, 4, lambda j: g_in(0, j).go(0))

            def early(j):
                g_in(1, j).go(0)
                d_in(1, j).go(0)

            def early_sent(j):
                g_in(1, j).sent_first()
                d_in(1, j).sent_first()

            at(tF + 8, NT - late, early_sent)
            at(tL + 4, late, lambda j: early_sent(NT - late + j))
            at(tF + 5, NT - late, early)

            @pl.when(t == tL)
            def _():
                def one(j, _):
                    early(j)
                    return 0

                lax.fori_loop(NT - late, NT, one, 0)

            at(tL + 1, 2 * NT, lambda u: start(rg_first(u)))
            at(tL + 5, 2 * NT, lambda v: start(rd_first(v) + own_loads(v)))

            @pl.when(t == 0)
            def _():
                start(own_x + own_w[0])
                acc[...] = jnp.zeros_like(acc)
                sg[...] = jnp.zeros_like(sg)
                sd[...] = jnp.zeros_like(sd)
                done(own_x)

                def begin(m, _):
                    r = ds(m * blk, blk, blk)
                    norm_into(0, r)
                    yT[:, r] = y[r, :].T
                    return 0

                lax.fori_loop(0, nblk, begin, 0)
                done(own_w[0])
                start(put_w[0])

            @pl.when(t == 1)
            def _():
                done(put_w[0])
                start(own_w[1])

            @pl.when(t == 2)
            def _():
                done(own_w[1])
                start(put_w[1])

            @pl.when(t == 3)
            def _():
                done(put_w[1])

            for l in range(layers):
                at(tF + l * NT - 1, NT, lambda j: g_in(l, j).go(4))
                at4(tF + l * NT - 1, lambda j: d_in(l, j).go(4))

            k = t + 1 - tF

            @pl.when((k >= 0) & (k < 3 * NT))
            def _():
                start(loads(lax.rem(lax.div(k, NT), 2), lax.rem(k, NT), k))

            @pl.when(t == tL)
            def _():
                def piece_(m, _):
                    r = ds(m * blk, blk, blk)
                    h[r, :] = (wide(h[r, :]) + wide(acc[r, :].astype(BF16))).astype(BF16)
                    acc[r, :] = jnp.zeros((blk, d), F32)
                    norm_into(1, r)
                    return 0

                lax.fori_loop(0, nblk, piece_, 0)

            @pl.when(t == tB)
            def _():
                def piece_(m, _):
                    r = ds(m * blk, blk, blk)
                    hw, da = wide(h[r, :]), wide(acc[r, :].astype(BF16))
                    scale = lax.rsqrt(jnp.mean(hw * hw, -1, keepdims=True) + 1e-6)
                    by_scale = jnp.sum(da * hw, -1, keepdims=True)
                    by_h = (da * scale - hw * (by_scale * scale * scale * scale * (1.0 / d))).astype(BF16)
                    by = (wide(y[r, :]) + wide(by_h)).astype(BF16)
                    y[r, :] = by
                    yT[:, r] = by.T
                    return 0

                lax.fori_loop(0, nblk, piece_, 0)

            def forward(j):
                s = lax.rem(j, 2)
                loaded(j)

                for m in range(tokens // span):
                    r = pl.ds(m * span, span)
                    both = nn(a[0, r, :], wgu_v[s])
                    gate, up = both[:, :TILE], both[:, TILE:]
                    p = (gate * (1 / (1 + jnp.exp(-gate))) * up).astype(BF16)
                    acc[r, :] += nn(p, wd_v[s])

            at(tF, NT, forward)

            def back_1(u):
                l, s = 1 - lax.div(u, NT), lax.rem(u + NT, 2)
                loaded(u + NT)

                for m in range(tokens // rows):
                    r = pl.ds(m * rows, rows)
                    both = nn(a[l, r, :], wgu_v[s])
                    gate, up = both[:, :TILE], both[:, TILE:]
                    by = wide(nt(y[r, :], wd_v[s]).astype(BF16))
                    sig = 1 / (1 + jnp.exp(-gate))
                    act = gate * sig
                    prod[r, :] = (act * up).astype(BF16)
                    dgu[r, TILE:] = (by * act).astype(BF16)
                    dgu[r, :TILE] = (by * up * (sig * (1 + gate * (1 - sig)))).astype(BF16)

            at(tL, 2 * NT, back_1)

            for k, ahead, more in ((3, 3, 1), (2, 4, 2), (1, 5, 3)):
                ramp(ahead, more, lambda j: g_in(0, j).go(k), k)
                if k == 2:
                    at4(tF - 3, lambda j: (d_in(0, j).go(2), d_in(0, j).go(3)))
                if k == 1:
                    at4(tF - 5, lambda j: d_in(0, j).go(1))
                at(tL - ahead - more, NT, lambda j: g_in(1, j).go(k))
                at4(tL - ahead - more, lambda j: d_in(1, j).go(k))

            def back_2(u):
                l, q = 1 - lax.div(u, NT), lax.rem(u, KEEP)

                dw[q] = nn(aT[l], dgu[...]).astype(BF16)

            at(tL, 2 * NT, back_2)

            def add_g(u):
                s, q = lax.rem(u, RING), lax.rem(u, KEEP)
                o = lax.rem(s, HELD)
                take_g(2 * half, rg_a.at[s])
                og[o, 0] = (wide(l1l[s]) + wide(dw[q, ds(right * dl, half), :])).astype(BF16)
                og[o, 1] = (wide(l1r[s]) + wide(dw[q, ds(left * dl + half, half), :])).astype(BF16)
                start(rg_next(u))

            def add_d(v):
                s = lax.rem(v, RING)
                o = lax.rem(s, HELD)
                take_d(2 * piece, rd_a.at[s])
                take_d(2 * piece, lown.at[0, s])
                od[o, 0] = (wide(k1l[s]) + wide(own[s, pl.ds(0, piece), :])).astype(BF16)
                od[o, 1] = (wide(k1r[s]) + wide(own[s, pl.ds(piece, piece), :])).astype(BF16)
                start(rd_next(v))

            at(tL + 2, 2 * NT, add_g)
            at(tL + 7, 2 * NT, add_d)

            def back_3(u):
                at_, s = dwd_out(u), lax.rem(u, 2)
                dwd[s] = nn(yT[...], prod[...]).astype(BF16).T
                start(at_)

            at(tL, 2 * NT, back_3)
            at(tL + 1, 2 * NT, lambda u: done(dwd_out(u)))

            def back_4(u):
                s = lax.rem(u + NT, 2)

                def part(m, _):
                    r = ds(m * span, span, span)
                    acc[r, :] += nt(dgu[r, :], wgu_v[s])
                    return 0

                lax.fori_loop(0, tokens // span, part, 0)

            at(tL, NT, back_4)

            def total_g(u):
                s, q, f = lax.rem(u, RING), lax.rem(u, KEEP), lax.rem(u, 2)
                take_g(4 * half, rg_b.at[s])
                lo = wide(dw[q, ds(me * dl, half), :]) + wide(l3l[s]) + wide(l2r[s])
                hi = wide(dw[q, ds(me * dl + half, half), :]) + wide(l3r[s]) + wide(l2l[s])
                lo, hi = lo.astype(BF16), hi.astype(BF16)
                fg[f, pl.ds(0, half), :] = lo
                fg[f, pl.ds(half, half), :] = hi
                lo, hi = wide(lo), wide(hi)
                sg[...] += jnp.sum((lo * lo + hi * hi).reshape(half // 8, 8, 2 * TILE), 0)
                start(g_out(u))
                take_g(6 * half, rg_s.at[s])

            def total_d(v):
                s, f = lax.rem(v, RING), lax.rem(v, 2)
                take_d(4 * piece, rd_b.at[s])
                take_d(2 * piece, lown.at[1, s])
                lo = wide(own[s, pl.ds(2 * piece, piece), :]) + wide(k3l[s]) + wide(k2r[s])
                hi = wide(own[s, pl.ds(3 * piece, piece), :]) + wide(k3r[s]) + wide(k2l[s])
                lo, hi = lo.astype(BF16), hi.astype(BF16)
                fd[f, pl.ds(0, piece), :] = lo
                fd[f, pl.ds(piece, piece), :] = hi
                lo, hi = wide(lo), wide(hi)
                sd[...] += jnp.sum((lo * lo + hi * hi).reshape(piece // 8, 8, d), 0)
                start(d_out(v))
                take_d(6 * piece, rd_s.at[s])

            at(tL + 5, 2 * NT, lambda u: take_g(dl, lout.at[0, lax.rem(u, 2)]))
            at(tL + 4, 2 * NT, total_g)
            at(tL + 10, 2 * NT, lambda v: done(d_out(v)))
            at(tL + 9, 2 * NT, total_d)
            return 0

        lax.fori_loop(0, end + 1, loop, 0)

        parts = [sg[:, k * 128 : (k + 1) * 128] for k in range(2 * TILE // 128)] + [sd[:, k * 128 : (k + 1) * 128] for k in range(d // 128)]
        st[3] = sum(parts[1:], parts[0])
        sends = [remote(st.at[3], st.at[k], st_s.at[k], st_r.at[k], to) for k, to in enumerate((R, L, O))]
        start(sends)
        done(sends)
        st[4] = st[0] + st[1] + st[2] + st[3]
        last = [local(st.at[4], stat, lin.at[0])]
        start(last)
        done(last)

    any_ = pl.BlockSpec(memory_space=pl.ANY)
    shapes = [
        ((layers, dl, ff), BF16), ((layers, dl, ff), BF16), ((layers, fl, d), BF16), ((8, 128), F32),
        ((layers, NT, d, 2 * TILE), BF16), ((layers, ff, d), BF16), ((layers, ff, d), BF16),
    ]
    V, S = pltpu.VMEM, pltpu.SemaphoreType.DMA
    scratch = [
        V((layers, tokens, d), BF16), V((layers, d, tokens), BF16), V((tokens, d), BF16), V((d, tokens), BF16), V((tokens, d), BF16),
        V((tokens, d), F32), V((tokens, TILE), BF16), V((tokens, 2 * TILE), BF16),
        V((2, d, 2 * TILE), BF16), V((2, TILE, d), BF16), V((KEEP, d, 2 * TILE), BF16), V((2, TILE, d), BF16),
        V((2, dl, 2 * TILE), BF16), V((2, 2 * piece, d), BF16), V((HELD, 2, half, 2 * TILE), BF16), V((HELD, 2, piece, d), BF16),
        V((RING, 4 * piece, d), BF16),
    ]
    scratch += [V((RING, half, 2 * TILE), BF16)] * 6 + [V((RING, piece, d), BF16)] * 6
    scratch += [V((8, 2 * TILE), F32), V((8, d), F32), V((5, 8, 128), F32)]
    way = [S((NT,)), S((3, TURNS)), S((layers, TURNS)), S((TURNS,))]
    scratch += way + way + [S((RING,))] * 6
    scratch += [S((2,)), S((2, RING)), S((2, 2)), S((2,)), S((3,)), S((3,)), S((3,))]
    return pl.pallas_call(
        body,
        out_shape=[jax.ShapeDtypeStruct(*s) for s in shapes],
        in_specs=[any_] * 5,
        out_specs=[any_] * 7,
        scratch_shapes=scratch,
        compiler_params=pltpu.CompilerParams(collective_id=0, has_side_effects=True, vmem_limit_bytes=67043328),
        name="exchange",
    )


def adamw(n, layers, dl, ff, fl, d):
    count = n * layers * (2 * dl * ff + fl * d)
    steps = 8

    def body(stat, *refs):
        ins, outs = refs[:12], refs[12:]
        factor = jnp.minimum(1.0, 0.5 * lax.rsqrt(jnp.sum(stat[...]) / count + 1e-30))
        for i in range(3):
            g, w, m, v = (ins[4 * i + k] for k in range(4))
            by = g[...].astype(F32) * factor
            first = 0.9 * m[...] + 0.1 * by
            second = 0.95 * v[...] + 0.05 * by * by
            old = w[...].astype(F32)
            outs[i][...] = (old - 0.02 * (first * lax.rsqrt(second + 1e-8) + 0.1 * old)).astype(BF16)
            outs[3 + i][...] = first
            outs[6 + i][...] = second

    sizes = [(layers * dl, ff), (layers * dl, ff), (layers * fl, d)]
    kinds = [pl.BlockSpec((rows // steps, columns), lambda i: (i, 0)) for rows, columns in sizes]
    call = pl.pallas_call(
        body,
        grid=(steps,),
        in_specs=[pl.BlockSpec((8, 128), lambda i: (0, 0))] + [k for k in kinds for _ in range(4)],
        out_specs=kinds * 3,
        out_shape=[jax.ShapeDtypeStruct(s, t) for t in (BF16, F32, F32) for s in sizes],
        compiler_params=pltpu.CompilerParams(vmem_limit_bytes=67043328),
        name="adamw",
    )

    def run(stat, gradients, weights, m, v):
        flat = [one.reshape(-1, one.shape[-1]) for four in zip(gradients, weights, m, v, strict=True) for one in four]
        shapes = [w.shape for w in weights] * 3
        return tuple(out.reshape(s) for out, s in zip(call(stat, *flat), shapes, strict=True))

    return run


def solution(mesh):
    n = mesh.shape["dp"]

    def step(x, dy, *arrays):
        weights, m, v = (arrays[i : i + 3] for i in (0, 3, 6))
        layers, ff, d = weights[2].shape[0], weights[2].shape[1] * n, weights[2].shape[2]
        *gradients, stat = exchange(n, x.shape[1], d, ff, layers)(x[0], dy[0], *weights)[:4]
        return adamw(n, layers, d // n, ff, ff // n, d)(stat, gradients, weights, m, v)

    states, cut = P(("rep", "dp"), None, None), P(None, "dp", None)
    return jax.shard_map(
        step,
        mesh=mesh,
        in_specs=(states, states) + (cut,) * 9,
        out_specs=(P("rep", "dp", None),) * 9,
        check_vma=False,
    )
```

time: 795 us -> 639 us (0.80)
  Pallas kernels: 740 us -> 638 us
  other arithmetic: 52 us -> 0 us
    pallas_call x1, Pallas kernels: 740 us -> 591 us  [step(): exchange(n, x.shape[1], d, ff, layers)(x[0], dy[0], *weights)[:4]]
    convert_element_type x2 -> x0, other arithmetic: 50.7 us -> none  [adamw(): return ((w - 0.02 * step).astype(BF16), m, v)]
    pallas_call x0 -> x1, Pallas kernels: none -> 46.6 us  [run(): call(stat, *flat)]
where the time goes in v2:
time: 639 us
  Pallas kernels  638 us (100%)
    pallas_call x1, Pallas kernels, step(): exchange(n, x.shape[1], d, ff, layers)(x[0], dy[0], *weights)[:4]  591 us
    pallas_call x1, Pallas kernels, run(): call(stat, *flat)  46.6 us

profile of v2, /device:TPU:112, one launch (start us, length us, event | category | flops | bytes accessed | tf_op | source)
XLA Modules:
  0.0 638.8 jit_solution(4064503912957897790)
XLA Ops:
  0.6 591.4 %exchange.1 = (bf16[2,224,4864]{2,1,0:T(8,128)(2,1)}, bf16[2,224,4864]{2,1,0:T(8,128)(2,1)}, bf16[2,1216,896]{2,1,0:T(8,128)(2,1)}, f32[8,128]{1,0:T(8,128)}, bf...) custom-call(bf16[2048,896]{1,0:T(8,128)(2,1)} %bitcast.35, ...), custom_call_target="tpu_custom_call" | custom-call | tf_op jit(solution)/shard_map/exchange/pallas_call | solution.py:566
  592.0 46.6 %adamw.1 = (bf16[448,4864]{1,0:T(8,128)(2,1)}, bf16[448,4864]{1,0:T(8,128)(2,1)}, bf16[2432,896]{1,0:T(8,128)(2,1)}, f32[448,4864]{1,0:T(8,128)}, f32[448,4864]{...) custom-call(f32[8,128]{1,0:T(8,128)} %get-tuple-element.22.stat, ...), custom_call_target="tpu_custom_call" | custom-call | tf_op jit(solution)/shard_map/adamw/pallas_call | solution.py:555

commit v3 on v2

--- a/solution.py
+++ b/solution.py
@@ -9,7 +9,7 @@
 TILE = 256
 RING = 8
 TURNS = 12
-KEEP = 5
+KEEP = 4
 HELD = 4
 
 
@@ -25,9 +25,10 @@
     assert n == 4 and layers == 2
     dl, fl, nt_ = d // n, ff // n, ff // TILE
     half, piece = dl // 2, fl // nt_ // 2
-    lent = (half * 3 // 7, half // 2)
-    lent_d = (0, piece // 2)
+    lent = (half * 2 // 7, half // 2)
+    lent_d = piece // 2
     rows, span = min(512, tokens), min(1024, tokens)
+    begin = 6
     late = 5
     NT = nt_
     m4 = NT - 3
@@ -75,8 +76,9 @@
             pltpu.make_async_copy(WD.at[0, pl.ds(0, rows_)], WD.at[0, pl.ds(0, rows_)], sem).wait()
 
         class Way:
-            def __init__(self, take, first, pass_on, share, whole, got, sent_a, sent_b, sizes):
+            def __init__(self, take, first, pass_on, share, whole, got, sent_a, sent_b, sizes, soon):
                 lo, hi = pass_on
+                self.soon = soon
                 self.take, self.got, self.sent_a, self.sent_b, self.sizes = take, got, sent_a, sent_b, sizes
                 self.first = [remote(src, dst, sent_a, got[0], to) for src, dst, to in first]
                 self.second = [remote(lo, lo, sent_b, got[1], R), remote(hi, hi, sent_b, got[1], L)]
@@ -86,7 +88,8 @@
             def go(self, step):
                 if step and self.sizes[step - 1]:
                     self.take(self.sizes[step - 1], self.got[step - 1])
-                start(((), self.second + self.across[:2], self.across[2:], self.inside, ())[step] if step else self.first)
+                k = 2 if self.soon else 0
+                start((self.first, self.second + self.across[:k], self.across[k:], self.inside, ())[step])
 
             def sent_first(self):
                 self.take(self.sizes[0], self.sent_a)
@@ -94,22 +97,22 @@
             def sent_rest(self):
                 self.take(sum(self.sizes[1:]), self.sent_b)
 
-        def d_in(l, j):
-            s, few = lax.rem(l * (NT + 1) + j, TURNS), lent_d[l]
-            most = piece - few
+        def d_in(l, j, many, few=lent_d):
+            s, few, part = lax.rem(l * (NT + 1) + j, TURNS), many * few, many * piece
+            most = part - few
 
             def rows_of(block, at, size):
-                return ds(block * fl + (2 * unit(block, j) + core) * piece + at, size, 8)
-
-            mine = wd.at[l, ds((2 * unit(me, j) + core) * piece + chip * few, most)]
+                return ds(block * fl + 2 * piece * unit(block, j) + part * core + at, size, 8)
+
+            mine = wd.at[l, ds(2 * piece * unit(me, j) + part * core + chip * few, most)]
             to = WD.at[l, rows_of(me, chip * few, most)]
             lo = WD.at[l, rows_of(left, chip * few, most // 2)]
             hi = WD.at[l, rows_of(right, chip * few + most // 2, most // 2)]
             share = lambda b: WD.at[l, rows_of(b, chip * most, few)]
-            whole = lambda b: WD.at[l, rows_of(b, 0, piece)]
+            whole = lambda b: WD.at[l, rows_of(b, 0, part)]
             got = [ad_1.at[j]] + [ad_n.at[i, s] for i in range(3)]
-            sizes = (2 * most, most, 3 * few, 3 * piece)
-            return Way(take_d, [(mine, to, R), (mine, to, L)], (lo, hi), share, whole, got, ad_a.at[l, lax.rem(j, TURNS)], ad_b.at[s], sizes)
+            sizes = (2 * most, most, 3 * few, 3 * part)
+            return Way(take_d, [(mine, to, R), (mine, to, L)], (lo, hi), share, whole, got, ad_a.at[l, lax.rem(j, TURNS)], ad_b.at[s], sizes, l == 0)
 
         def g_in(l, j):
             s, few = lax.rem(l * NT + j, TURNS), lent[l]
@@ -129,7 +132,7 @@
             whole = lambda b: WGU.at[l, j, rows_of(b, 0, half)]
             got = [ag_1.at[j]] + [ag_n.at[i, s] for i in range(3)]
             sizes = (2 * most, most, 3 * few, 3 * half)
-            return Way(take_g, first, (lo, hi), share, whole, got, ag_a.at[l, lax.rem(j, TURNS)], ag_b.at[s], sizes)
+            return Way(take_g, first, (lo, hi), share, whole, got, ag_a.at[l, lax.rem(j, TURNS)], ag_b.at[s], sizes, l == 0)
 
         def loads(l, j, k):
             s = lax.rem(k, 2)
@@ -215,7 +218,7 @@
 
         tF = 7
         tL, tB, tE = tF + NT, tF + 2 * NT, tF + 3 * NT
-        end = tE + 9
+        end = tE + 8
         blk = min(256, tokens)
         nblk = tokens // blk
 
@@ -231,110 +234,113 @@
             a[l, r, :] = n_
             aT[l, :, r] = n_.T
 
-        def loop(t, _):
+        def loop(t, lo_, hi_):
+            def when(*terms, within=(0, end + 1)):
+                if within[0] >= hi_ or within[1] <= lo_:
+                    return lambda f: None
+                if within[0] <= lo_ and within[1] >= hi_ and not terms:
+                    return lambda f: f()
+                test = (t >= within[0]) & (t < within[1])
+                for term in terms:
+                    test = test & term
+                return pl.when(test)
+
             def at(t0, count, f):
-                k = t - t0
-
-                @pl.when((k >= 0) & (k < count))
-                def _():
-                    f(k)
+                when(*([t >= 0] if f in products else []), within=(t0, t0 + count))(lambda: f(t - t0))
+
+            products = []
+
+            def product(f):
+                products.append(f)
+                return f
+
+            def once(t0):
+                return when(within=(t0, t0 + 1))
 
             def ramp(ahead, more, f, late=0):
-                lo, hi = (jnp.clip(s - tF + ahead + jnp.clip(s - tF - late, 0, more), 0, NT) for s in (t, t + 1))
-
-                @pl.when(hi > lo)
-                def _():
-                    def one(j, _):
-                        f(j)
-                        return 0
-
-                    lax.fori_loop(lo, hi, one, 0)
-
-            def at4(t0, f):
-                k = t - t0
-
-                @pl.when((k >= 0) & (k < NT) & (lax.rem(k, 4) == 0))
-                def _():
-                    def one(v, _):
-                        f(v)
-                        return 0
-
-                    lax.fori_loop(k, jnp.minimum(k + 4, NT), one, 0)
+                lo, hi = (
+                    jnp.clip(s - tF + ahead + jnp.clip(s - tF - late, 0, more) - jnp.where((s == tF) & (late == 3), 1, 0), 0, NT) for s in (t, t + 1)
+                )
+
+                when(hi > lo + 1, within=(tF - ahead, tL))(lambda: f(lo))
+                when(hi > lo, within=(tF - ahead, tL))(lambda: f(hi - 1))
+
+            def at4(l, first, then, f, only=None):
+                if only != "then":
+                    once(first)(lambda: f(d_in(l, 0, 4, 0)))
+                if only != "first":
+                    k = t - then
+                    when(lax.rem(k, 4) == 0, within=(then + 1, then + m4))(lambda: f(d_in(l, k, 4)))
+
+                    @once(then + m4)
+                    def _():
+                        def one(v, _):
+                            f(d_in(l, v, 1))
+                            return 0
+
+                        lax.fori_loop(m4, NT, one, 0)
 
             at(tF - 4, NT, lambda j: g_in(0, j).sent_first())
-            at4(tF - 4, lambda j: d_in(0, j).sent_first())
+            at4(0, tF - 4, tF - 4, lambda w: w.sent_first())
             for l in range(layers):
                 at(tF + l * NT + 1, NT, lambda j: g_in(l, j).sent_rest())
-                at4(tF + l * NT, lambda j: d_in(l, j).sent_rest())
-            at4(tF - 7, lambda j: d_in(0, j).go(0))
+                at4(l, tF + l * NT, tF + l * NT, lambda w: w.sent_rest())
+            at4(0, tF - 7, tF - 8, lambda w: w.go(0))
             ramp(6, 4, lambda j: g_in(0, j).go(0))
 
-            def early(j):
-                g_in(1, j).go(0)
-                d_in(1, j).go(0)
-
-            def early_sent(j):
-                g_in(1, j).sent_first()
-                d_in(1, j).sent_first()
-
-            at(tF + 8, NT - late, early_sent)
-            at(tL + 4, late, lambda j: early_sent(NT - late + j))
-            at(tF + 5, NT - late, early)
-
-            @pl.when(t == tL)
+            at(tF + begin + 4, NT - late, lambda j: g_in(1, j).sent_first())
+            at(tL + 4, late, lambda j: g_in(1, NT - late + j).sent_first())
+            at4(1, tF + begin + 4, tF + begin + 4, lambda w: w.sent_first())
+            at(tF + begin, NT - late, lambda j: g_in(1, j).go(0))
+            at4(1, tF + begin, tF + begin, lambda w: w.go(0))
+
+            @once(tL)
             def _():
                 def one(j, _):
-                    early(j)
+                    g_in(1, j).go(0)
                     return 0
 
                 lax.fori_loop(NT - late, NT, one, 0)
 
-            at(tL + 1, 2 * NT, lambda u: start(rg_first(u)))
-            at(tL + 5, 2 * NT, lambda v: start(rd_first(v) + own_loads(v)))
-
-            @pl.when(t == 0)
+            at(tL + 1, 2 * NT, lambda u: done(dwd_out(u)))
+            at(tL + 4, 2 * NT, lambda v: start(rd_first(v) + own_loads(v)))
+
+            @once(0)
             def _():
                 start(own_x + own_w[0])
                 acc[...] = jnp.zeros_like(acc)
                 sg[...] = jnp.zeros_like(sg)
                 sd[...] = jnp.zeros_like(sd)
+
+            @once(1)
+            def _():
                 done(own_x)
 
-                def begin(m, _):
+                def start_on(m, _):
                     r = ds(m * blk, blk, blk)
                     norm_into(0, r)
                     yT[:, r] = y[r, :].T
                     return 0
 
-                lax.fori_loop(0, nblk, begin, 0)
+                lax.fori_loop(0, nblk, start_on, 0)
                 done(own_w[0])
                 start(put_w[0])
 
-            @pl.when(t == 1)
+            @once(2)
             def _():
                 done(put_w[0])
                 start(own_w[1])
 
-            @pl.when(t == 2)
+            @once(3)
             def _():
                 done(own_w[1])
                 start(put_w[1])
 
-            @pl.when(t == 3)
+            @once(4)
             def _():
                 done(put_w[1])
 
-            for l in range(layers):
-                at(tF + l * NT - 1, NT, lambda j: g_in(l, j).go(4))
-                at4(tF + l * NT - 1, lambda j: d_in(l, j).go(4))
-
-            k = t + 1 - tF
-
-            @pl.when((k >= 0) & (k < 3 * NT))
-            def _():
-                start(loads(lax.rem(lax.div(k, NT), 2), lax.rem(k, NT), k))
-
-            @pl.when(t == tL)
+            @once(tL)
             def _():
                 def piece_(m, _):
                     r = ds(m * blk, blk, blk)
@@ -345,7 +351,7 @@
 
                 lax.fori_loop(0, nblk, piece_, 0)
 
-            @pl.when(t == tB)
+            @once(tB)
             def _():
                 def piece_(m, _):
                     r = ds(m * blk, blk, blk)
@@ -360,6 +366,19 @@
 
                 lax.fori_loop(0, nblk, piece_, 0)
 
+            for l in range(layers):
+                at(tF + l * NT - 1, NT, lambda j: g_in(l, j).go(4))
+
+            for l in range(layers):
+                at4(l, tF + l * NT - 1, tF + l * NT - 1, lambda w: w.go(4))
+
+            k = t + 1 - tF
+
+            @when(within=(tF - 1, tE - 1))
+            def _():
+                start(loads(lax.rem(lax.div(k, NT), 2), lax.rem(k, NT), k))
+
+            @product
             def forward(j):
                 s = lax.rem(j, 2)
                 loaded(j)
@@ -373,6 +392,7 @@
 
             at(tF, NT, forward)
 
+            @product
             def back_1(u):
                 l, s = 1 - lax.div(u, NT), lax.rem(u + NT, 2)
                 loaded(u + NT)
@@ -390,15 +410,15 @@
 
             at(tL, 2 * NT, back_1)
 
-            for k, ahead, more in ((3, 3, 1), (2, 4, 2), (1, 5, 3)):
+            for k, ahead, more, ahead_0, ahead_d, ahead_1 in ((3, 3, 1, 3, 3, 2), (2, 4, 2, 3, 4, 6), (1, 5, 3, 5, 6, 8)):
                 ramp(ahead, more, lambda j: g_in(0, j).go(k), k)
+                at4(0, tF - ahead_0, tF - ahead_d, lambda w: w.go(k), "then" if k == 3 else None)
                 if k == 2:
-                    at4(tF - 3, lambda j: (d_in(0, j).go(2), d_in(0, j).go(3)))
-                if k == 1:
-                    at4(tF - 5, lambda j: d_in(0, j).go(1))
-                at(tL - ahead - more, NT, lambda j: g_in(1, j).go(k))
-                at4(tL - ahead - more, lambda j: d_in(1, j).go(k))
-
+                    at4(0, tF - ahead_0, tF - ahead_d, lambda w: w.go(3), "first")
+                at(tL - ahead_1, NT, lambda j: g_in(1, j).go(k))
+                at4(1, tL - ahead_1, tL - ahead_1, lambda w: w.go(k))
+
+            @product
             def back_2(u):
                 l, q = 1 - lax.div(u, NT), lax.rem(u, KEEP)
 
@@ -406,6 +426,7 @@
 
             at(tL, 2 * NT, back_2)
 
+            @product
             def add_g(u):
                 s, q = lax.rem(u, RING), lax.rem(u, KEEP)
                 o = lax.rem(s, HELD)
@@ -414,6 +435,7 @@
                 og[o, 1] = (wide(l1r[s]) + wide(dw[q, ds(left * dl + half, half), :])).astype(BF16)
                 start(rg_next(u))
 
+            @product
             def add_d(v):
                 s = lax.rem(v, RING)
                 o = lax.rem(s, HELD)
@@ -423,17 +445,19 @@
                 od[o, 1] = (wide(k1r[s]) + wide(own[s, pl.ds(piece, piece), :])).astype(BF16)
                 start(rd_next(v))
 
-            at(tL + 2, 2 * NT, add_g)
-            at(tL + 7, 2 * NT, add_d)
-
+            at(tL + 1, 2 * NT, add_g)
+            at(tL + 6, 2 * NT, add_d)
+
+            @product
             def back_3(u):
                 at_, s = dwd_out(u), lax.rem(u, 2)
                 dwd[s] = nn(yT[...], prod[...]).astype(BF16).T
                 start(at_)
 
             at(tL, 2 * NT, back_3)
-            at(tL + 1, 2 * NT, lambda u: done(dwd_out(u)))
-
+            at(tL, 2 * NT, lambda u: start(rg_first(u)))
+
+            @product
             def back_4(u):
                 s = lax.rem(u + NT, 2)
 
@@ -446,6 +470,7 @@
 
             at(tL, NT, back_4)
 
+            @product
             def total_g(u):
                 s, q, f = lax.rem(u, RING), lax.rem(u, KEEP), lax.rem(u, 2)
                 take_g(4 * half, rg_b.at[s])
@@ -459,6 +484,7 @@
                 start(g_out(u))
                 take_g(6 * half, rg_s.at[s])
 
+            @product
             def total_d(v):
                 s, f = lax.rem(v, RING), lax.rem(v, 2)
                 take_d(4 * piece, rd_b.at[s])
@@ -473,13 +499,18 @@
                 start(d_out(v))
                 take_d(6 * piece, rd_s.at[s])
 
-            at(tL + 5, 2 * NT, lambda u: take_g(dl, lout.at[0, lax.rem(u, 2)]))
-            at(tL + 4, 2 * NT, total_g)
-            at(tL + 10, 2 * NT, lambda v: done(d_out(v)))
-            at(tL + 9, 2 * NT, total_d)
-            return 0
-
-        lax.fori_loop(0, end + 1, loop, 0)
+            at(tL + 4, 2 * NT, lambda u: take_g(dl, lout.at[0, lax.rem(u, 2)]))
+            at(tL + 3, 2 * NT, total_g)
+            at(tL + 9, 2 * NT, lambda v: done(d_out(v)))
+            at(tL + 8, 2 * NT, total_d)
+
+        for lo_, hi_ in ((0, tF), (tF, tL), (tL, tB), (tB, tE), (tE, end + 1)):
+
+            def step(t, _, lo_=lo_, hi_=hi_):
+                loop(t, lo_, hi_)
+                return 0
+
+            lax.fori_loop(lo_, hi_, step, 0)
 
         parts = [sg[:, k * 128 : (k + 1) * 128] for k in range(2 * TILE // 128)] + [sd[:, k * 128 : (k + 1) * 128] for k in range(d // 128)]
         st[3] = sum(parts[1:], parts[0])

time: 639 us -> 629 us (0.984)
  Pallas kernels: 638 us -> 627 us
    pallas_call x1, Pallas kernels: 591 us -> 580 us  [step(): exchange(n, x.shape[1], d, ff, layers)(x[0], dy[0], *weights)[:4]]
where the time goes in v3:
time: 629 us; the launch traced here: 628 us
  Pallas kernels  627 us (100%)
    pallas_call x1, Pallas kernels, step(): exchange(n, x.shape[1], d, ff, layers)(x[0], dy[0], *weights)[:4]  580 us
    pallas_call x1, Pallas kernels, run(): call(stat, *flat)  46.6 us

profile of v3, /device:TPU:112, one launch (start us, length us, event | category | flops | bytes accessed | tf_op | source)
XLA Modules:
  0.0 627.8 jit_solution(15552476212611637806)
XLA Ops:
  0.6 580.4 %exchange.1 = (bf16[2,224,4864]{2,1,0:T(8,128)(2,1)}, bf16[2,224,4864]{2,1,0:T(8,128)(2,1)}, bf16[2,1216,896]{2,1,0:T(8,128)(2,1)}, f32[8,128]{1,0:T(8,128)}, bf...) custom-call(bf16[2048,896]{1,0:T(8,128)(2,1)} %bitcast.35, ...), custom_call_target="tpu_custom_call" | custom-call | tf_op jit(solution)/shard_map/exchange/pallas_call | solution.py:597
  581.0 46.6 %adamw.1 = (bf16[448,4864]{1,0:T(8,128)(2,1)}, bf16[448,4864]{1,0:T(8,128)(2,1)}, bf16[2432,896]{1,0:T(8,128)(2,1)}, f32[448,4864]{1,0:T(8,128)}, f32[448,4864]{...) custom-call(f32[8,128]{1,0:T(8,128)} %get-tuple-element.22.stat, ...), custom_call_target="tpu_custom_call" | custom-call | tf_op jit(solution)/shard_map/adamw/pallas_call | solution.py:586

commit v4 on v3

--- a/solution.py
+++ b/solution.py
@@ -345,7 +345,6 @@
                 def piece_(m, _):
                     r = ds(m * blk, blk, blk)
                     h[r, :] = (wide(h[r, :]) + wide(acc[r, :].astype(BF16))).astype(BF16)
-                    acc[r, :] = jnp.zeros((blk, d), F32)
                     norm_into(1, r)
                     return 0
 
@@ -410,7 +409,7 @@
 
             at(tL, 2 * NT, back_1)
 
-            for k, ahead, more, ahead_0, ahead_d, ahead_1 in ((3, 3, 1, 3, 3, 2), (2, 4, 2, 3, 4, 6), (1, 5, 3, 5, 6, 8)):
+            for k, ahead, more, ahead_0, ahead_d, ahead_1 in ((3, 3, 1, 3, 3, 2), (2, 4, 2, 3, 4, 4), (1, 5, 3, 5, 6, 8)):
                 ramp(ahead, more, lambda j: g_in(0, j).go(k), k)
                 at4(0, tF - ahead_0, tF - ahead_d, lambda w: w.go(k), "then" if k == 3 else None)
                 if k == 2:
@@ -463,7 +462,7 @@
 
                 def part(m, _):
                     r = ds(m * span, span, span)
-                    acc[r, :] += nt(dgu[r, :], wgu_v[s])
+                    acc[r, :] = nt(dgu[r, :], wgu_v[s]) + jnp.where(u > 0, acc[r, :], 0.0)
                     return 0
 
                 lax.fori_loop(0, tokens // span, part, 0)

time: 629 us -> 628 us (level)
  no operation moved by 1% of the time
where the time goes in v4:
time: 628 us; the launch traced here: 627 us
  Pallas kernels  626 us (100%)
    pallas_call x1, Pallas kernels, step(): exchange(n, x.shape[1], d, ff, layers)(x[0], dy[0], *weights)[:4]  580 us
    pallas_call x1, Pallas kernels, run(): call(stat, *flat)  46.6 us

profile of v4, /device:TPU:112, one launch (start us, length us, event | category | flops | bytes accessed | tf_op | source)
XLA Modules:
  0.0 627.2 jit_solution(18372766900355006663)
XLA Ops:
  0.6 579.8 %exchange.1 = (bf16[2,224,4864]{2,1,0:T(8,128)(2,1)}, bf16[2,224,4864]{2,1,0:T(8,128)(2,1)}, bf16[2,1216,896]{2,1,0:T(8,128)(2,1)}, f32[8,128]{1,0:T(8,128)}, bf...) custom-call(bf16[2048,896]{1,0:T(8,128)(2,1)} %bitcast.35, ...), custom_call_target="tpu_custom_call" | custom-call | tf_op jit(solution)/shard_map/exchange/pallas_call | solution.py:596
  580.4 46.6 %adamw.1 = (bf16[448,4864]{1,0:T(8,128)(2,1)}, bf16[448,4864]{1,0:T(8,128)(2,1)}, bf16[2432,896]{1,0:T(8,128)(2,1)}, f32[448,4864]{1,0:T(8,128)}, f32[448,4864]{...) custom-call(f32[8,128]{1,0:T(8,128)} %get-tuple-element.22.stat, ...), custom_call_target="tpu_custom_call" | custom-call | tf_op jit(solution)/shard_map/adamw/pallas_call | solution.py:585
